TPU v7x, 1024 devices: a whole 4x4x32 slice. The times are simulated.
1024 devices in a mesh: sfc: 256 (over x, z, core), lvl: 4 (over y).
Axes of the slice: x: 4, y: 4, z: 32, core: 2. Of those that a mesh axis runs over, the one named last changes fastest.
Arguments:
- right_side: float32 [524288, 128], P(('sfc', 'lvl')), may hold values from -48 to 48
- cell_coef: float32 [524288], P(('sfc', 'lvl')), may hold values from 4 to 16
- fine_count: int32 [1024], replicated, may hold values from 256 to 512, as said below
- cell_matrix: float32 [128, 128], replicated, may hold values from -0.5 to 0.5
- face_near: float32 [128, 128], replicated, may hold values from -0.5 to 0.5
- face_far: float32 [128, 128], replicated, may hold values from -0.5 to 0.5
- prolong: float32 [8, 128, 128], replicated, may hold values from -0.5 to 0.5
Outputs:
- solution: float32 [524288, 128], P(('sfc', 'lvl'))
Inputs may be any that keep to these rules, and one draw needn't show every extreme that they name: `fine_count`: each device's count is a multiple of 8 and at least 256; exactly one device holds 512, every other at most 504.
All inputs are finite; a program needn't handle non-finite values.
Results may differ from a plain program's by a relative error of at most 0.000051.
Values sent between devices are 32-bit elements; how exact they have to be, the bound alone decides.
A program may use at most 32 MiB of HBM per device.

v0:
```python
import jax
import jax.numpy as jnp
from jax import lax
from jax.sharding import PartitionSpec as P

DEG = 3


def with_halo(shard, sides, width):
    edges = {}
    for axis, dim in sides:
        size, length = (lax.axis_size(axis), shard.shape[dim])
        up = [(i, (i + 1) % size) for i in range(size - 1)]
        last = lax.slice_in_dim(shard, length - width, length, axis=dim)
        leading = lax.slice_in_dim(shard, 0, width, axis=dim)
        edges[dim] = (
            lax.ppermute(last, axis, up),
            lax.ppermute(leading, axis, [(b, a) for a, b in up]),
        )
    done = []
    for _, dim in sides:
        low, high = edges[dim]
        around = [(width, width) if d in done else (0, 0) for d in range(shard.ndim)]
        shard = jnp.concatenate([jnp.pad(low, around), shard, jnp.pad(high, around)], axis=dim)
        done.append(dim)
    return shard


def padded(cells, sides, width):
    for axis, dim in sides:
        count = lax.axis_size(axis)
        ends = count - 1
        head = lax.slice_in_dim(cells, 0, width, axis=dim)
        tail = lax.slice_in_dim(cells, cells.shape[dim] - width, cells.shape[dim], axis=dim)
        cells = jnp.concatenate(
            [
                lax.ppermute(tail, axis, [(i, (i + 1) % count) for i in range(ends)]),
                cells,
                lax.ppermute(head, axis, [((i + 1) % count, i) for i in range(ends)]),
            ],
            axis=dim,
        )
    return cells


def chain_apply(field, chain_coef, is_live, live_count, stride, ghosts, coupling):
    capacity = field.shape[0]
    tail_rows = lax.dynamic_slice_in_dim(field, live_count - stride, stride, 0)
    rim_rows = jnp.concatenate([field[:stride], tail_rows], 0)
    extended = ghosts(rim_rows)
    ghost_prev = extended[:stride]
    ghost_next = extended[3 * stride :]
    buffer = jnp.concatenate(
        [ghost_prev, field, jnp.zeros((stride, field.shape[1]), jnp.float32)], 0
    )
    buffer = lax.dynamic_update_slice_in_dim(buffer, ghost_next, stride + live_count, 0)
    joined = jnp.concatenate(
        [
            field,
            buffer[stride + 1 : stride + 1 + capacity],
            buffer[stride - 1 : stride - 1 + capacity],
            buffer[2 * stride : 2 * stride + capacity],
            buffer[:capacity],
        ],
        1,
    )
    result = chain_coef[:, None] * field + jnp.dot(
        joined, coupling, precision=lax.Precision.HIGHEST, preferred_element_type=jnp.float32
    )
    return jnp.where(is_live[:, None], result, 0.0)


def local_apply(field, chain_coef, is_live, stride, coupling):
    width = field.shape[1]
    zero_one = jnp.zeros((1, width), jnp.float32)
    zero_far = jnp.zeros((stride, width), jnp.float32)
    joined = jnp.concatenate(
        [
            field,
            jnp.concatenate([field[1:], zero_one], 0),
            jnp.concatenate([zero_one, field[:-1]], 0),
            jnp.concatenate([field[stride:], zero_far], 0),
            jnp.concatenate([zero_far, field[:-stride]], 0),
        ],
        1,
    )
    result = chain_coef[:, None] * field + jnp.dot(
        joined, coupling, precision=lax.Precision.HIGHEST, preferred_element_type=jnp.float32
    )
    return jnp.where(is_live[:, None], result, 0.0)


def rims_of(field, live_count, depth):
    tail_rows = lax.dynamic_slice_in_dim(field, live_count - depth, depth, 0)
    return jnp.concatenate([field[:depth], tail_rows], 0)


def widen(field, ghost_rows, live_count, depth):
    tail_zeros = jnp.zeros((depth,) + field.shape[1:], jnp.float32)
    buffer = jnp.concatenate([ghost_rows[:depth], field, tail_zeros], 0)
    return lax.dynamic_update_slice_in_dim(buffer, ghost_rows[3 * depth :], depth + live_count, 0)


def jacobi_scale(chain_coef, is_live, cell_diag):
    safe_coef = jnp.where(is_live, chain_coef, 16.0)
    return jnp.where(is_live[:, None], 1.0 / (safe_coef[:, None] + cell_diag[None, :]), 0.0)


def chebyshev(apply_fn, jacobi, source, start):
    center = 1.025
    radius = 0.775
    sigma_ratio = center / radius
    if start is None:
        residual = source
    else:
        residual = source - apply_fn(start)
    update = jacobi * residual / center
    iterate = update if start is None else start + update
    weight_prev = 1.0 / sigma_ratio
    for repeat in range(DEG - 1):
        weight_next = 1.0 / (2.0 * sigma_ratio - weight_prev)
        residual = source - apply_fn(iterate)
        update = weight_next * weight_prev * update + 2.0 * weight_next / radius * jacobi * residual
        iterate = iterate + update
        weight_prev = weight_next
    return iterate


def shards(right_side, cell_coef, fine_count, cell_matrix, face_near, face_far, prolong):
    capacity, values = right_side.shape
    stride = capacity // 16
    coarse_stride = capacity // 16
    coarse_slots = capacity // 8
    coupling = jnp.concatenate([cell_matrix, -face_near, -face_near.T, -face_far, -face_far.T], 0)
    cell_diag = jnp.diagonal(cell_matrix)
    device_index = lax.axis_index(("sfc", "lvl"))
    live_count = fine_count[device_index]
    is_live = jnp.arange(capacity, dtype=jnp.int32) < live_count
    source = jnp.where(is_live[:, None], right_side, 0.0)
    depth = 3 * stride
    chain_size = lax.axis_size(("sfc", "lvl"))
    wide_index = jnp.arange(capacity + 2 * depth, dtype=jnp.int32)
    has_prev = device_index > 0
    has_next = device_index < chain_size - 1
    wide_live = (
        (wide_index >= depth) & (wide_index < depth + live_count)
        | (wide_index < depth) & has_prev
        | (wide_index >= depth + live_count) & (wide_index < 2 * depth + live_count) & has_next
    )
    own_coef = jnp.where(is_live, cell_coef, 0.0)
    source_ghosts = with_halo(rims_of(source, live_count, depth), ((("sfc", "lvl"), 0),), depth)
    coef_ghosts = with_halo(rims_of(own_coef, live_count, depth), ((("sfc", "lvl"), 0),), depth)
    wide_source = widen(source, source_ghosts, live_count, depth)
    wide_coef = widen(own_coef, coef_ghosts, live_count, depth)
    wide_jacobi = jacobi_scale(wide_coef, wide_live, cell_diag)

    def wide_apply(field):
        return local_apply(field, wide_coef, wide_live, stride, coupling)

    wide_iterate = chebyshev(wide_apply, wide_jacobi, wide_source, None)
    wide_residual = wide_source - wide_apply(wide_iterate)
    iterate = jnp.where(is_live[:, None], wide_iterate[depth : depth + capacity], 0.0)
    residual = jnp.where(is_live[:, None], wide_residual[depth : depth + capacity], 0.0)
    restrict_map = jnp.transpose(prolong, (0, 2, 1)).reshape(8 * values, values)
    coarse_source = jnp.dot(
        residual.reshape(coarse_slots, 8 * values),
        restrict_map,
        precision=lax.Precision.HIGHEST,
        preferred_element_type=jnp.float32,
    )
    coarse_coef = jnp.mean(cell_coef.reshape(coarse_slots, 8), axis=1)
    coarse_count = live_count // 8
    is_coarse = jnp.arange(coarse_slots, dtype=jnp.int32) < coarse_count
    coarse_jacobi = jacobi_scale(coarse_coef, is_coarse, cell_diag)

    def spread_ghosts(rim_rows):
        return with_halo(rim_rows, ((("sfc", "lvl"), 0),), coarse_stride)

    def spread_apply(field):
        return chain_apply(
            field, coarse_coef, is_coarse, coarse_count, coarse_stride, spread_ghosts, coupling
        )

    correction = chebyshev(spread_apply, coarse_jacobi, coarse_source, None)
    prolong_map = jnp.transpose(prolong, (1, 0, 2)).reshape(values, 8 * values)
    corrected = iterate + jnp.dot(
        correction, prolong_map, precision=lax.Precision.HIGHEST, preferred_element_type=jnp.float32
    ).reshape(capacity, values)
    start_ghosts = padded(rims_of(corrected, live_count, depth), ((("sfc", "lvl"), 0),), depth)
    wide_start = widen(corrected, start_ghosts, live_count, depth)
    wide_final = chebyshev(wide_apply, wide_jacobi, wide_source, wide_start)
    return jnp.where(is_live[:, None], wide_final[depth : depth + capacity], 0.0)


def solution(mesh):
    placed = (P(("sfc", "lvl"), None), P(("sfc", "lvl")), P(), P(), P(), P(), P())
    return jax.shard_map(
        shards, mesh=mesh, in_specs=placed, out_specs=P(("sfc", "lvl"), None), check_vma=False
    )
```

profile of v0, /device:TPU:6, one launch (start us, length us, event | category | flops | bytes accessed | tf_op | source)
XLA Modules:
  0.0 98.3 jit_solution(16653527467936838085)
XLA Ops:
  0.0 1.3 %dynamic_slice.18 = s32[1]{0:T(128)} dynamic-slice(s32[1024]{0:T(1024)} %param.9, s32[]{:T(128)S(6)} %select_n.91), dynamic_slice_sizes={1} | dynamic-slice | bytes 12 | tf_op jit(solution)/shard_map/dynamic_slice | solution.py:137
  1.3 1.3 %broadcast_select_fusion.2 = f32[512]{0:T(512)S(1)} fusion(f32[512]{0:T(512)} %param.8, s32[]{:T(128)} %bitcast), kind=kLoop, calls=%fused_computation.104 | loop fusion | flops 1024 | bytes 4100 | tf_op jit(solution)/shard_map/jit(_where)/select_n | solution.py:150
  4.0 3.5 %collective-permute-start = (f32[96]{0:T(128)S(1)}, f32[96]{0:T(128)S(1)}, u32[]{:S(2)}, u32[]{:S(2)}) collective-permute-start(f32[96]{0:T(128)S(1)} %get-tuple-element.59), channel_id=1, source_target_pairs={{0,1},{1,2},{2,3},{3,4},{4,5},{5,6},{6,7},{7,8},{8,9},{9,10},{10,1... | collective-permute-start | bytes 1160 | tf_op jit(solution)/shard_map/ppermute | solution.py:17
  7.5 19.3 %collective-permute-start.1 = (f32[96]{0:T(128)S(1)}, f32[96]{0:T(128)S(1)}, u32[]{:S(2)}, u32[]{:S(2)}) collective-permute-start(f32[96]{0:T(128)S(1)} %get-tuple-element.58), channel_id=1, source_target_pairs={{1,0},{2,1},{3,2},{4,3},{5,4},{6,5},{7,6},{8,7},{9,8},{10,9},{11,1... | collective-permute-start | bytes 1160 | tf_op jit(solution)/shard_map/ppermute | solution.py:18
  26.8 0.7 iota_compare_fusion.5
  27.5 1.1 %broadcast_select_fusion = f32[512,128]{1,0:T(8,128)S(1)} fusion(f32[512,128]{1,0:T(8,128)} %param.7, pred[512]{0:T(512)(128)(4,1)S(1)} %iota_compare_fusion.5), kind=kLoop, calls=%fused_computation.58 | loop fusion | flops 65536 | bytes 524800 | tf_op jit(solution)/shard_map/jit(_where)/select_n | solution.py:139
  28.6 1.9 %collective-permute-start.2 = (f32[96,128]{1,0:T(8,128)S(1)}, f32[96,128]{1,0:T(8,128)S(1)}, u32[]{:S(2)}, u32[]{:S(2)}) collective-permute-start(f32[96,128]{1,0:T(8,128)S(1)} %get-tuple-element.49), channel_id=1, source_target_pairs={{0,1},{1,2},{2,3},{3,4},{4,5},{5,6},{6,7},{7,8},{8,9},{9,10},{10,1... | collective-permute-start | bytes 147464 | tf_op jit(solution)/shard_map/ppermute | solution.py:17
  30.5 7.9 %collective-permute-start.3 = (f32[96,128]{1,0:T(8,128)S(1)}, f32[96,128]{1,0:T(8,128)S(1)}, u32[]{:S(2)}, u32[]{:S(2)}) collective-permute-start(f32[96,128]{1,0:T(8,128)S(1)} %get-tuple-element.48), channel_id=1, source_target_pairs={{1,0},{2,1},{3,2},{4,3},{5,4},{6,5},{7,6},{8,7},{9,8},{10,9},{11,1... | collective-permute-start | bytes 147464 | tf_op jit(solution)/shard_map/ppermute | solution.py:18
  38.4 0.8 reshape.52
  42.4 1.2 %copy.14 = f32[8,128,128]{1,2,0:T(8,128)S(1)} copy(f32[8,128,128]{2,1,0:T(8,128)} %param.13) | data formatting | bytes 1048576 | tf_op args[6]
  43.7 1.2 %gather_fusion = f32[128]{0:T(128)S(1)} fusion(f32[128,128]{1,0:T(8,128)S(1)} %copy-done, s32[128]{0:T(128)S(1)} %or_bitcast_fusion), kind=kCustom, calls=%fused_computation | custom fusion | bytes 2048 | tf_op jit(solution)/shard_map/jit(diagonal)/cond/branch_0_fun/gather | solution.py:135
  47.4 0.5 dynamic_update_slice.16
  48.4 1.8 %constant_dynamic-update-slice_fusion.6 = (f32[704,640]{1,0:T(8,128)S(1)}, f32[704,128]{1,0:T(8,128)S(1)}, f32[704,128]{1,0:T(8,128)S(1)}) fusion(f32[704,128]{1,0:T(8,128)S(1)} %get-tuple-element.19, f32[704,128]{1,0:T(8,128)S(1)} %dynamic_update_slice.16, f32[704]{0:T(1024)S(1)} %get-tuple-element.57, f32[128]{0:T(128)S(1)} %gather_fusion, ...), kind=kOutput, calls=%fused_computation.65 | convolution fusion | flops 693231616 | bytes 3939008 | tf_op jit(solution)/shard_map/dot_general | solution.py:87
  50.5 1.8 %constant_dynamic-update-slice_fusion.7 = (f32[704,640]{1,0:T(8,128)S(1)}, f32[704,128]{1,0:T(8,128)S(1)}, f32[704,128]{1,0:T(8,128)S(1)}) fusion(f32[704,128]{1,0:T(8,128)S(1)} %get-tuple-element.17, f32[704,128]{1,0:T(8,128)S(1)} %dynamic_update_slice.16, f32[704]{0:T(1024)S(1)} %dynamic_update_slice.15, f32[704,128]{1,0:T(8,128)S(1)} %get-tuple-element.65, ...), kind=kOutput, calls=%fused_computation.66 | convolution fusion | flops 693952512 | bytes 4302272 | tf_op jit(solution)/shard_map/dot_general | solution.py:87
  52.6 1.6 %fusion.48 = f32[704,128]{1,0:T(8,128)S(1)} fusion(f32[704,640]{1,0:T(8,128)S(1)} %pad_dynamic-update-slice_fusion.12, f32[640,128]{1,0:T(8,128)S(1)} %constant_dynamic-update-slice_fusion.1), kind=kOutput, calls=%fused_computation.135 | convolution fusion | flops 692060160 | bytes 2490368 | tf_op jit(solution)/shard_map/dot_general | solution.py:87
  54.5 0.4 constant_dynamic-update-slice_fusion.12
  55.0 1.9 %collective-permute-start.4 = (f32[32,128]{1,0:T(8,128)S(1)}, f32[32,128]{1,0:T(8,128)S(1)}, u32[]{:S(2)}, u32[]{:S(2)}) collective-permute-start(f32[32,128]{1,0:T(8,128)S(1)} %get-tuple-element.55), channel_id=1, source_target_pairs={{0,1},{1,2},{2,3},{3,4},{4,5},{5,6},{6,7},{7,8},{8,9},{9,10},{10,1... | collective-permute-start | bytes 49160 | tf_op jit(solution)/shard_map/ppermute | solution.py:17
  57.0 7.8 %collective-permute-start.5 = (f32[32,128]{1,0:T(8,128)S(1)}, f32[32,128]{1,0:T(8,128)S(1)}, u32[]{:S(2)}, u32[]{:S(2)}) collective-permute-start(f32[32,128]{1,0:T(8,128)S(1)} %get-tuple-element.54), channel_id=1, source_target_pairs={{1,0},{2,1},{3,2},{4,3},{5,4},{6,5},{7,6},{8,7},{9,8},{10,9},{11,1... | collective-permute-start | bytes 49160 | tf_op jit(solution)/shard_map/ppermute | solution.py:18
  64.9 1.3 %collective-permute-done.5 = f32[32,128]{1,0:T(8,128)S(1)} collective-permute-done((f32[32,128]{1,0:T(8,128)S(1)}, f32[32,128]{1,0:T(8,128)S(1)}, u32[]{:S(2)}, u32[]{:S(2)}) %collective-permute-start.5) | collective-permute-done | bytes 16416 | tf_op jit(solution)/shard_map/ppermute | solution.py:18
  66.5 0.3 constant_dynamic-update-slice_fusion.17
  66.8 1.9 %collective-permute-start.6 = (f32[32,128]{1,0:T(8,128)S(1)}, f32[32,128]{1,0:T(8,128)S(1)}, u32[]{:S(2)}, u32[]{:S(2)}) collective-permute-start(f32[32,128]{1,0:T(8,128)S(1)} %get-tuple-element.53), channel_id=1, source_target_pairs={{0,1},{1,2},{2,3},{3,4},{4,5},{5,6},{6,7},{7,8},{8,9},{9,10},{10,1... | collective-permute-start | bytes 49160 | tf_op jit(solution)/shard_map/ppermute | solution.py:17
  68.8 7.9 %collective-permute-start.7 = (f32[32,128]{1,0:T(8,128)S(1)}, f32[32,128]{1,0:T(8,128)S(1)}, u32[]{:S(2)}, u32[]{:S(2)}) collective-permute-start(f32[32,128]{1,0:T(8,128)S(1)} %get-tuple-element.52), channel_id=1, source_target_pairs={{1,0},{2,1},{3,2},{4,3},{5,4},{6,5},{7,6},{8,7},{9,8},{10,9},{11,1... | collective-permute-start | bytes 49160 | tf_op jit(solution)/shard_map/ppermute | solution.py:18
  76.7 1.3 %collective-permute-done.7 = f32[32,128]{1,0:T(8,128)S(1)} collective-permute-done((f32[32,128]{1,0:T(8,128)S(1)}, f32[32,128]{1,0:T(8,128)S(1)}, u32[]{:S(2)}, u32[]{:S(2)}) %collective-permute-start.7) | collective-permute-done | bytes 16416 | tf_op jit(solution)/shard_map/ppermute | solution.py:18
  78.6 0.7 fusion.14
  79.5 1.9 %collective-permute-start.8 = (f32[96,128]{1,0:T(8,128)S(1)}, f32[96,128]{1,0:T(8,128)S(1)}, u32[]{:S(2)}, u32[]{:S(2)}) collective-permute-start(f32[96,128]{1,0:T(8,128)S(1)} %get-tuple-element.47), channel_id=1, source_target_pairs={{0,1},{1,2},{2,3},{3,4},{4,5},{5,6},{6,7},{7,8},{8,9},{9,10},{10,1... | collective-permute-start | bytes 147464 | tf_op jit(solution)/shard_map/ppermute | solution.py:37
  81.4 8.0 %collective-permute-start.9 = (f32[96,128]{1,0:T(8,128)S(1)}, f32[96,128]{1,0:T(8,128)S(1)}, u32[]{:S(2)}, u32[]{:S(2)}) collective-permute-start(f32[96,128]{1,0:T(8,128)S(1)} %get-tuple-element.46), channel_id=1, source_target_pairs={{1,0},{2,1},{3,2},{4,3},{5,4},{6,5},{7,6},{8,7},{9,8},{10,9},{11,1... | collective-permute-start | bytes 147464 | tf_op jit(solution)/shard_map/ppermute | solution.py:39
  89.6 1.4 %collective-permute-done.9 = f32[96,128]{1,0:T(8,128)S(1)} collective-permute-done((f32[96,128]{1,0:T(8,128)S(1)}, f32[96,128]{1,0:T(8,128)S(1)}, u32[]{:S(2)}, u32[]{:S(2)}) %collective-permute-start.9) | collective-permute-done | bytes 49184 | tf_op jit(solution)/shard_map/ppermute | solution.py:39
  91.0 0.4 dynamic_update_slice.19
  91.7 1.8 %constant_dynamic-update-slice_fusion.19 = (f32[704,640]{1,0:T(8,128)S(1)}, f32[704,128]{1,0:T(8,128)S(1)}, f32[704,128]{1,0:T(8,128)S(1)}) fusion(f32[704,128]{1,0:T(8,128)S(1)} %dynamic_update_slice.19, f32[704,128]{1,0:T(8,128)S(1)} %dynamic_update_slice.16, f32[704]{0:T(1024)S(1)} %dynamic_update_slice.15, f32[128]{0:T(128)S(1)} %gather_fusion, ...), kind=kOutput, calls=%fused_computation.78 | convolution fusion | flops 692961280 | bytes 3939008 | tf_op jit(solution)/shard_map/dot_general | solution.py:87
  93.7 1.8 %broadcast_multiply_fusion = (f32[704,128]{1,0:T(8,128)S(1)}, f32[704,128]{1,0:T(8,128)S(1)}, f32[704,128]{1,0:T(8,128)S(1)}) fusion(f32[704]{0:T(1024)S(1)} %dynamic_update_slice.15, f32[704,128]{1,0:T(8,128)S(1)} %get-tuple-element.9, f32[704,128]{1,0:T(8,128)S(1)} %dynamic_update_slice.16, f32[704,128]{1,0:T(8,128)S(1)} %get-tuple-element.68, ...), kind=kOutput, calls=%fused_computation.56 | convolution fusion | flops 693682176 | bytes 4659904 | tf_op jit(solution)/shard_map/dot_general | solution.py:87
  95.8 1.6 %fusion.49 = f32[704,128]{1,0:T(8,128)S(1)} fusion(f32[704,640]{1,0:T(8,128)S(1)} %pad_dynamic-update-slice_fusion, f32[640,128]{1,0:T(8,128)S(1)} %constant_dynamic-update-slice_fusion.1), kind=kOutput, calls=%fused_computation.136 | convolution fusion | flops 692060160 | bytes 2490368 | tf_op jit(solution)/shard_map/dot_general | solution.py:87
  97.4 0.9 fusion.7
  (97 shorter events, 4.3 us)
Async XLA Ops:
  0.0 43.6 %copy-start = (f32[128,128]{1,0:T(8,128)S(1)}, f32[128,128]{1,0:T(8,128)}, u32[]{:S(2)}) copy-start(f32[128,128]{1,0:T(8,128)} %param.10) | copy-start | bytes 196612
  0.0 46.4 %copy-start.2 = (f32[128,128]{1,0:T(8,128)S(1)}, f32[128,128]{1,0:T(8,128)}, u32[]{:S(2)}) copy-start(f32[128,128]{1,0:T(8,128)} %param.11) | copy-start | bytes 196612
  0.0 46.6 %copy-start.1 = (f32[128,128]{1,0:T(8,128)S(1)}, f32[128,128]{1,0:T(8,128)}, u32[]{:S(2)}) copy-start(f32[128,128]{1,0:T(8,128)} %param.12) | copy-start | bytes 196612
  4.0 42.8 %collective-permute-start = (f32[96]{0:T(128)S(1)}, f32[96]{0:T(128)S(1)}, u32[]{:S(2)}, u32[]{:S(2)}) collective-permute-start(f32[96]{0:T(128)S(1)} %get-tuple-element.59), channel_id=1, source_target_pairs={{0,1},{1,2},{2,3},{3,4},{4,5},{5,6},{6,7},{7,8},{8,9},{9,10},{10,1... | collective-permute-start | bytes 1160 | tf_op jit(solution)/shard_map/ppermute | solution.py:17
  7.5 39.4 %collective-permute-start.1 = (f32[96]{0:T(128)S(1)}, f32[96]{0:T(128)S(1)}, u32[]{:S(2)}, u32[]{:S(2)}) collective-permute-start(f32[96]{0:T(128)S(1)} %get-tuple-element.58), channel_id=1, source_target_pairs={{1,0},{2,1},{3,2},{4,3},{5,4},{6,5},{7,6},{8,7},{9,8},{10,9},{11,1... | collective-permute-start | bytes 1160 | tf_op jit(solution)/shard_map/ppermute | solution.py:18
  28.6 18.7 %collective-permute-start.2 = (f32[96,128]{1,0:T(8,128)S(1)}, f32[96,128]{1,0:T(8,128)S(1)}, u32[]{:S(2)}, u32[]{:S(2)}) collective-permute-start(f32[96,128]{1,0:T(8,128)S(1)} %get-tuple-element.49), channel_id=1, source_target_pairs={{0,1},{1,2},{2,3},{3,4},{4,5},{5,6},{6,7},{7,8},{8,9},{9,10},{10,1... | collective-permute-start | bytes 147464 | tf_op jit(solution)/shard_map/ppermute | solution.py:17
  30.5 16.9 %collective-permute-start.3 = (f32[96,128]{1,0:T(8,128)S(1)}, f32[96,128]{1,0:T(8,128)S(1)}, u32[]{:S(2)}, u32[]{:S(2)}) collective-permute-start(f32[96,128]{1,0:T(8,128)S(1)} %get-tuple-element.48), channel_id=1, source_target_pairs={{1,0},{2,1},{3,2},{4,3},{5,4},{6,5},{7,6},{8,7},{9,8},{10,9},{11,1... | collective-permute-start | bytes 147464 | tf_op jit(solution)/shard_map/ppermute | solution.py:18
  55.0 9.9 %collective-permute-start.4 = (f32[32,128]{1,0:T(8,128)S(1)}, f32[32,128]{1,0:T(8,128)S(1)}, u32[]{:S(2)}, u32[]{:S(2)}) collective-permute-start(f32[32,128]{1,0:T(8,128)S(1)} %get-tuple-element.55), channel_id=1, source_target_pairs={{0,1},{1,2},{2,3},{3,4},{4,5},{5,6},{6,7},{7,8},{8,9},{9,10},{10,1... | collective-permute-start | bytes 49160 | tf_op jit(solution)/shard_map/ppermute | solution.py:17
  57.0 9.3 %collective-permute-start.5 = (f32[32,128]{1,0:T(8,128)S(1)}, f32[32,128]{1,0:T(8,128)S(1)}, u32[]{:S(2)}, u32[]{:S(2)}) collective-permute-start(f32[32,128]{1,0:T(8,128)S(1)} %get-tuple-element.54), channel_id=1, source_target_pairs={{1,0},{2,1},{3,2},{4,3},{5,4},{6,5},{7,6},{8,7},{9,8},{10,9},{11,1... | collective-permute-start | bytes 49160 | tf_op jit(solution)/shard_map/ppermute | solution.py:18
  66.8 9.8 %collective-permute-start.6 = (f32[32,128]{1,0:T(8,128)S(1)}, f32[32,128]{1,0:T(8,128)S(1)}, u32[]{:S(2)}, u32[]{:S(2)}) collective-permute-start(f32[32,128]{1,0:T(8,128)S(1)} %get-tuple-element.53), channel_id=1, source_target_pairs={{0,1},{1,2},{2,3},{3,4},{4,5},{5,6},{6,7},{7,8},{8,9},{9,10},{10,1... | collective-permute-start | bytes 49160 | tf_op jit(solution)/shard_map/ppermute | solution.py:17
  68.8 9.3 %collective-permute-start.7 = (f32[32,128]{1,0:T(8,128)S(1)}, f32[32,128]{1,0:T(8,128)S(1)}, u32[]{:S(2)}, u32[]{:S(2)}) collective-permute-start(f32[32,128]{1,0:T(8,128)S(1)} %get-tuple-element.52), channel_id=1, source_target_pairs={{1,0},{2,1},{3,2},{4,3},{5,4},{6,5},{7,6},{8,7},{9,8},{10,9},{11,1... | collective-permute-start | bytes 49160 | tf_op jit(solution)/shard_map/ppermute | solution.py:18
  79.5 10.0 %collective-permute-start.8 = (f32[96,128]{1,0:T(8,128)S(1)}, f32[96,128]{1,0:T(8,128)S(1)}, u32[]{:S(2)}, u32[]{:S(2)}) collective-permute-start(f32[96,128]{1,0:T(8,128)S(1)} %get-tuple-element.47), channel_id=1, source_target_pairs={{0,1},{1,2},{2,3},{3,4},{4,5},{5,6},{6,7},{7,8},{8,9},{9,10},{10,1... | collective-permute-start | bytes 147464 | tf_op jit(solution)/shard_map/ppermute | solution.py:37
  81.4 9.6 %collective-permute-start.9 = (f32[96,128]{1,0:T(8,128)S(1)}, f32[96,128]{1,0:T(8,128)S(1)}, u32[]{:S(2)}, u32[]{:S(2)}) collective-permute-start(f32[96,128]{1,0:T(8,128)S(1)} %get-tuple-element.46), channel_id=1, source_target_pairs={{1,0},{2,1},{3,2},{4,3},{5,4},{6,5},{7,6},{8,7},{9,8},{10,9},{11,1... | collective-permute-start | bytes 147464 | tf_op jit(solution)/shard_map/ppermute | solution.py:39
where the time goes:
time: 98.9 us; the launch traced here: 98.3 us
  starting transfers between devices  62 us (63%)
  matrix products  12.2 us (12%)
  local copies, waits for them, and re-layouts  7.98 us (8%)
  between operations  6.74 us (7%)
  other arithmetic  5.35 us (5%)
  waiting for transfers between devices  4.05 us (4%)
    ppermute x4, starting transfers between devices, with_halo(): lax.ppermute(leading, axis, [(b, a) for a, b in up])  42.8 us
    dot_general x6, matrix products, local_apply(): jnp.dot(joined, coupling, precision=lax.Precision.HIGHEST, preferred_elem...  10.4 us
    ppermute x4, starting transfers between devices, with_halo(): lax.ppermute(last, axis, up)  9.23 us
    ppermute x1, starting transfers between devices, padded(): lax.ppermute(head, axis, [((i + 1) % count, i) for i in range(ends)])  8.04 us
    ppermute x4, waiting for transfers between devices, with_halo(): lax.ppermute(leading, axis, [(b, a) for a, b in up])  2.66 us
  transfers between devices with their start and end apart: 10, of which 3 were waited for; matrix products, arithmetic and copies ran while one was open for 7% of the time, Pallas kernels for 0%

commit v1 on v0

v1 whole, which is shorter than its diff:
```python
import functools

import jax
import jax.numpy as jnp
from jax import lax
from jax.experimental import pallas as pl
from jax.experimental.pallas import tpu as pltpu
from jax.sharding import PartitionSpec as P

DEG = 3
CENTER = 1.025
RADIUS = 0.775
STEPS = (1, -1, 2, -2, 3, -3)
F32 = jnp.float32
BF16 = jnp.bfloat16


def weights_of():
    ratio = CENTER / RADIUS
    prev = 1.0 / ratio
    pairs = []
    for _ in range(DEG - 1):
        new = 1.0 / (2.0 * ratio - prev)
        pairs.append((new * prev, 2.0 * new / RADIUS))
        prev = new
    return pairs


def split(x):
    high = x.astype(BF16)
    low = (x - high.astype(F32)).astype(BF16)
    return high, low


def rows_of(start, size):
    return start + lax.broadcasted_iota(jnp.int32, (size, 128), 0)


def columns(row):
    return jnp.transpose(jnp.broadcast_to(row, (128, 128)))


def cycle(
    n, lanes, cap,
    counts_hbm, b_hbm, coef_hbm, cell_hbm, near_hbm, far_hbm, prolong_hbm,
    out_ref,
    counts, b_own, coef, cell, near, far, prolong,
    tail, ghost_low, ghost_high, meta, meta_in,
    a_left, a_high, wide_b, wide_a, wide_j, x, d, y, res,
    main_w, low_w, rest_w, rest_low, pro_w, pro_low,
    c_own, c_tail, c_coef, l1, l2, l3, r1, r2, r3, k1, k2, k3, q1, q2, q3,
    c_b, c_a, c_j, c_x, c_d,
    local_sem, b_send, b_recv, m_send, m_recv, c_send, c_recv,
):
    stride = cap // 16
    depth = 5 * stride
    total = cap + 2 * depth
    c_cap = cap // 8
    base = c_cap + 16
    c_total = base + c_cap + base
    half = cap // 2
    me = lax.axis_index("sfc") * lanes + lax.axis_index("lvl")

    def at(step):
        return lax.rem(me + (step + n), n)

    def device(step):
        t = at(step)
        return (lax.div(t, lanes), lax.rem(t, lanes))

    barrier = pltpu.get_barrier_semaphore()
    for s in STEPS:
        pl.semaphore_signal(
            barrier, inc=1, device_id=device(s), device_id_type=pl.DeviceIdType.MESH
        )
    loads = [
        pltpu.make_async_copy(src, dst, local_sem.at[i])
        for i, (src, dst) in enumerate(
            [
                (counts_hbm, counts), (coef_hbm, coef), (b_hbm, b_own), (cell_hbm, cell),
                (near_hbm, near), (far_hbm, far), (prolong_hbm, prolong),
            ]
        )
    ]
    for c in loads:
        c.start()

    def remote(src, dst, send, recv, slot):
        return pltpu.make_async_remote_copy(
            src_ref=src, dst_ref=dst, send_sem=send.at[slot], recv_sem=recv.at[slot],
            device_id=device(STEPS[slot]), device_id_type=pl.DeviceIdType.MESH,
        )

    loads[0].wait()
    loads[1].wait()
    def count(t):
        return jnp.minimum(jnp.maximum(counts[t], half), cap)

    live = count(me)
    c_live = lax.div(live, 8)
    for i in range(cap // 128):
        wide_a[pl.ds(depth + 128 * i, 128), :] = columns(coef[pl.ds(i, 1), :])
    mean = wide_a[pl.ds(depth, c_cap, stride=8), :]
    for c in range(1, 8):
        mean = mean + wide_a[pl.ds(depth + c, c_cap, stride=8), :]
    mean = mean * 0.125
    c_coef[pl.ds(0, c_cap), :] = jnp.zeros((c_cap, 128), F32)
    c_coef[pl.ds(c_cap, c_cap), :] = mean
    c_own[pl.ds(0, c_cap), :] = jnp.zeros((c_cap, 128), F32)
    both = jnp.concatenate([mean, c_coef[pl.ds(c_live, c_cap), :]], 0)
    meta[pl.ds(0, 4), :] = coef[...]
    meta[pl.ds(4, 4), :] = jnp.transpose(both)[0:4, :]

    loads[2].wait()
    tail[...] = b_own[pl.ds(8 * (c_live - depth // 8), depth), :]
    pl.semaphore_wait(barrier, len(STEPS))
    halo = [
        remote(tail, ghost_low, b_send, b_recv, 0),
        remote(b_own.at[pl.ds(0, depth)], ghost_high.at[pl.ds(half, depth)], b_send, b_recv, 1),
    ]
    metas = [
        remote(meta, meta_in.at[i], m_send, m_recv, i) for i in range(len(STEPS))
    ]
    metas[0].start()
    metas[1].start()
    for c in halo:
        c.start()
    for c in metas[2:]:
        c.start()

    for c in loads[3:6]:
        c.wait()
    near_m = near[...]
    far_m = far[...]
    cell_m = cell[...]
    blocks = [cell_m, -near_m, -jnp.transpose(near_m), -far_m, -jnp.transpose(far_m)]
    for i, m in enumerate(blocks):
        high, low = split(m)
        main_w[pl.ds(0, 128), pl.ds(128 * i, 128)] = high
        main_w[pl.ds(128, 128), pl.ds(128 * i, 128)] = high
        low_w[:, pl.ds(128 * i, 128)] = low
    eye = lax.broadcasted_iota(jnp.int32, (128, 128), 0) == lax.broadcasted_iota(
        jnp.int32, (128, 128), 1
    )
    diag = jnp.sum(jnp.where(eye, cell_m, 0.0), axis=0, keepdims=True)
    loads[6].wait()
    for i in range(8):
        m = prolong[i]
        high, low = split(m)
        pro_w[pl.ds(0, 128), pl.ds(128 * i, 128)] = high
        pro_w[pl.ds(128, 128), pl.ds(128 * i, 128)] = high
        pro_low[:, pl.ds(128 * i, 128)] = low
        high, low = split(jnp.transpose(m))
        rest_w[pl.ds(256 * i, 128), :] = high
        rest_w[pl.ds(256 * i + 128, 128), :] = high
        rest_low[pl.ds(128 * i, 128), :] = low
    y[:, pl.ds(0, stride), :] = jnp.zeros((5, stride, 128), F32)
    y[:, pl.ds(stride + total, stride), :] = jnp.zeros((5, stride, 128), F32)

    for c in metas:
        c.wait_recv()
    for i in range(cap // 128):
        a_left[pl.ds(128 * i, 128), :] = columns(meta_in[0, pl.ds(i, 1), :])
    for i in range(2):
        a_high[pl.ds(half + 128 * i, 128), :] = columns(meta_in[1, pl.ds(i, 1), :])
    for i, (ref, at_row, first, size) in enumerate(
        [
            (k1, 16, 128 - c_cap, c_cap), (q1, 32, 0, c_cap),
            (k2, 0, 128 - 48, 48), (q2, 64, 0, 48),
            (k3, 0, 128 - 16, 16), (q3, 96, 0, 16),
        ]
    ):
        ref[pl.ds(at_row, size), :] = columns(meta_in[i, pl.ds(4, 1), :])[first : first + size]

    has_prev = me > 0
    has_next = me < n - 1
    left_live = count(at(-1))
    low_limit = jnp.where(has_prev, 0, depth)
    high_limit = depth + live + jnp.where(has_next, depth, 0)
    shift = 8 * (cap // 8 - c_live)
    n1 = lax.div(left_live, 8)
    a_low = a_left[pl.ds(8 * (n1 - depth // 8), depth), :]
    own_a = wide_a[pl.ds(depth + half, half), :]
    more_a = a_high[pl.ds(shift, cap + depth - half), :]
    index = rows_of(depth + half, cap + depth - half)
    inside = index < depth + live
    wide_a[pl.ds(0, depth), :] = jnp.where(rows_of(0, depth) >= low_limit, a_low, 0.0)
    padded_a = jnp.concatenate([own_a, jnp.zeros((depth, 128), F32)], 0)
    wide_a[pl.ds(depth + half, cap + depth - half), :] = jnp.where(
        index < high_limit, jnp.where(inside, padded_a, more_a), 0.0
    )
    all_rows = rows_of(0, total)
    is_live = (all_rows >= low_limit) & (all_rows < high_limit)
    wide_j[...] = jnp.where(is_live, 1.0 / (jnp.where(is_live, wide_a[...], 16.0) + diag), 0.0)

    for c in halo:
        c.wait_recv()
    wide_b[pl.ds(0, depth), :] = jnp.where(
        rows_of(0, depth) >= low_limit, ghost_low[...], 0.0
    )
    wide_b[pl.ds(depth, half), :] = b_own[pl.ds(0, half), :]
    padded_b = jnp.concatenate(
        [b_own[pl.ds(half, half), :], jnp.zeros((depth, 128), F32)], 0
    )
    more_b = ghost_high[pl.ds(shift, cap + depth - half), :]
    wide_b[pl.ds(depth + half, cap + depth - half), :] = jnp.where(
        index < high_limit, jnp.where(inside, padded_b, more_b), 0.0
    )

    def products(field, low, high):
        first, size = low - stride, high - low + 2 * stride
        hi, lo = split(field[pl.ds(first, size), :])
        pair = jnp.concatenate([hi, lo], 1)
        for start in range(0, 640, 256):
            width = min(256, 640 - start)
            part = jnp.dot(
                pair, main_w[:, pl.ds(start, width)], preferred_element_type=F32
            ) + jnp.dot(hi, low_w[:, pl.ds(start, width)], preferred_element_type=F32)
            for k in range(width // 128):
                y[start // 128 + k, pl.ds(stride + first, size), :] = part[
                    :, 128 * k : 128 * k + 128
                ]

    def applied(field, coefs, low, high):
        size = high - low
        row = stride + low
        return (
            coefs[pl.ds(low, size), :] * field[pl.ds(low, size), :]
            + y[0, pl.ds(row, size), :]
            + y[1, pl.ds(row + 1, size), :]
            + y[2, pl.ds(row - 1, size), :]
            + y[3, pl.ds(row + stride, size), :]
            + y[4, pl.ds(row - stride, size), :]
        )

    def residual(field, coefs, source, low, high):
        products(field, low, high)
        return source[pl.ds(low, high - low), :] - applied(field, coefs, low, high)

    def improve(field, update, coefs, scale, source, low, high, keep, gain):
        rows = pl.ds(low, high - low)
        r = residual(field, coefs, source, low, high)
        step = gain * scale[rows, :] * r
        if keep is not None:
            step = keep * update[rows, :] + step
        update[rows, :] = step
        field[rows, :] = field[rows, :] + step

    pairs = weights_of()
    first = wide_j[...] * wide_b[...] * (1.0 / CENTER)
    x[...] = first
    d[...] = first
    low, high = stride, total - stride
    for keep, gain in pairs:
        improve(x, d, wide_a, wide_j, wide_b, low, high, keep, gain)
        low, high = low + stride, high - stride
    res[...] = residual(x, wide_a, wide_b, depth, depth + cap)

    acc = jnp.zeros((c_cap, 128), F32)
    for i in range(8):
        hi, lo = split(res[pl.ds(i, c_cap, stride=8), :])
        acc = acc + jnp.dot(
            jnp.concatenate([hi, lo], 1), rest_w[pl.ds(256 * i, 256), :],
            preferred_element_type=F32,
        )
        acc = acc + jnp.dot(hi, rest_low[pl.ds(128 * i, 128), :], preferred_element_type=F32)
    c_own[pl.ds(c_cap, c_cap), :] = acc
    c_tail[...] = c_own[pl.ds(c_live, c_cap), :]
    coarse = [
        remote(c_tail, l1.at[pl.ds(16, c_cap)], c_send, c_recv, 0),
        remote(c_own.at[pl.ds(c_cap, c_cap)], r1.at[pl.ds(32, c_cap)], c_send, c_recv, 1),
        remote(c_tail.at[pl.ds(c_cap - 48, 48)], l2.at[pl.ds(0, 48)], c_send, c_recv, 2),
        remote(c_own.at[pl.ds(c_cap, 48)], r2.at[pl.ds(64, 48)], c_send, c_recv, 3),
        remote(c_tail.at[pl.ds(c_cap - 16, 16)], l3.at[pl.ds(0, 16)], c_send, c_recv, 4),
        remote(c_own.at[pl.ds(c_cap, 16)], r3.at[pl.ds(96, 16)], c_send, c_recv, 5),
    ]
    for c in coarse:
        c.start()

    n2 = lax.div(count(at(-2)), 8)
    p1 = lax.div(count(at(1)), 8)
    p2 = lax.div(count(at(2)), 8)
    e2 = base - n1
    e3 = e2 - n2
    s1 = base + c_live
    s2 = s1 + p1
    s3 = s2 + p2
    c_low = jnp.where(
        me >= 3, e3 - 16, jnp.where(me == 2, e3, jnp.where(me == 1, e2, base))
    )
    c_high = jnp.where(
        me + 3 < n, s3 + 16, jnp.where(me + 3 == n, s3, jnp.where(me + 2 == n, s2, s1))
    )

    def gathered(target, own, b1, b2, b3, a1, a2, a3):
        r = rows_of(0, base)
        v2 = jnp.concatenate([b2[pl.ds(48 - e2, 48), :], jnp.zeros((base - 48, 128), F32)], 0)
        v3 = jnp.concatenate([b3[pl.ds(16 - e3, 16), :], jnp.zeros((base - 16, 128), F32)], 0)
        value = jnp.where(r >= e2, b1[...], jnp.where(r >= e3, v2, v3))
        target[pl.ds(0, base), :] = jnp.where(r >= c_low, value, 0.0)
        r = rows_of(base, c_cap + base)
        v0 = jnp.concatenate([own, jnp.zeros((base, 128), F32)], 0)
        v1 = jnp.concatenate([jnp.zeros((32, 128), F32), a1[pl.ds(c_cap - c_live, 112), :]], 0)
        v2 = jnp.concatenate([jnp.zeros((64, 128), F32), a2[pl.ds(208 - s2, 80), :]], 0)
        v3 = jnp.concatenate([jnp.zeros((96, 128), F32), a3[pl.ds(272 - s3, 48), :]], 0)
        value = jnp.where(
            r < s1, v0, jnp.where(r < s2, v1, jnp.where(r < s3, v2, v3))
        )
        target[pl.ds(base, c_cap + base), :] = jnp.where(r < c_high, value, 0.0)

    gathered(c_a, mean, k1, k2, k3, q1, q2, q3)
    r = rows_of(0, c_total)
    c_live_rows = (r >= c_low) & (r < c_high)
    c_j[...] = jnp.where(
        c_live_rows, 1.0 / (jnp.where(c_live_rows, c_a[...], 16.0) + diag), 0.0
    )
    for c in coarse:
        c.wait_recv()
    gathered(c_b, acc, l1, l2, l3, r1, r2, r3)
    first = c_j[...] * c_b[...] * (1.0 / CENTER)
    c_x[...] = first
    c_d[...] = first
    for i, (keep, gain) in enumerate(pairs):
        low = stride * (i + 1)
        improve(c_x, c_d, c_a, c_j, c_b, low, c_total - low, keep, gain)

    rows = c_cap + 32
    hi, lo = split(c_x[pl.ds(base - 16, rows), :])
    pair = jnp.concatenate([hi, lo], 1)
    for start in range(0, 1024, 256):
        part = jnp.dot(
            pair, pro_w[:, pl.ds(start, 256)], preferred_element_type=F32
        ) + jnp.dot(hi, pro_low[:, pl.ds(start, 256)], preferred_element_type=F32)
        for k in range(2):
            where = pl.ds(depth - 128 + start // 128 + k, rows, stride=8)
            x[where, :] = x[where, :] + part[:, 128 * k : 128 * k + 128]

    low, high = depth - 2 * stride, depth + cap + 2 * stride
    improve(x, d, wide_a, wide_j, wide_b, low, high, None, 1.0 / CENTER)
    for keep, gain in pairs:
        low, high = low + stride, high - stride
        improve(x, d, wide_a, wide_j, wide_b, low, high, keep, gain)
    out_ref[...] = jnp.where(rows_of(0, cap) < live, x[pl.ds(depth, cap), :], 0.0)
    for c in halo + metas + coarse:
        c.wait_send()


def shards(n, lanes, right_side, cell_coef, fine_count, cell_matrix, face_near, face_far, prolong):
    cap = right_side.shape[0]
    stride = cap // 16
    depth = 5 * stride
    total = cap + 2 * depth
    c_cap = cap // 8
    base = c_cap + 16
    c_total = 2 * base + c_cap
    half = cap // 2

    def vmem(*shape, dtype=F32):
        return pltpu.VMEM(shape, dtype)

    scratch = [
        pltpu.SMEM(fine_count.shape, jnp.int32), vmem(cap, 128), vmem(4, 128),
        vmem(128, 128), vmem(128, 128), vmem(128, 128), vmem(8, 128, 128),
        vmem(depth, 128), vmem(depth, 128), vmem(cap + depth, 128), vmem(8, 128),
        vmem(6, 8, 128),
        vmem(cap, 128), vmem(cap + depth, 128), vmem(total, 128), vmem(total, 128),
        vmem(total, 128), vmem(total, 128), vmem(total, 128),
        vmem(5, total + 2 * stride, 128), vmem(cap, 128),
        vmem(256, 640, dtype=BF16), vmem(128, 640, dtype=BF16),
        vmem(2048, 128, dtype=BF16), vmem(1024, 128, dtype=BF16),
        vmem(256, 1024, dtype=BF16), vmem(128, 1024, dtype=BF16),
        vmem(2 * c_cap, 128), vmem(c_cap, 128), vmem(2 * c_cap, 128),
    ]
    for _ in range(2):
        scratch += [vmem(base, 128)] * 3 + [vmem(base + c_cap, 128)] * 3
    scratch += [vmem(c_total, 128)] * 5
    dma = pltpu.SemaphoreType.DMA
    scratch += [dma((7,)), dma((2,)), dma((2,)), dma((6,)), dma((6,)), dma((6,)), dma((6,))]
    return pl.pallas_call(
        functools.partial(cycle, n, lanes, cap),
        out_shape=jax.ShapeDtypeStruct(right_side.shape, F32),
        in_specs=[pl.BlockSpec(memory_space=pl.ANY)] * 7,
        out_specs=pl.BlockSpec(memory_space=pltpu.VMEM),
        scratch_shapes=scratch,
        compiler_params=pltpu.CompilerParams(collective_id=0, has_side_effects=True),
        name="cycle",
    )(
        fine_count, right_side, cell_coef.reshape(4, 128), cell_matrix, face_near, face_far,
        prolong,
    )


def solution(mesh):
    placed = (P(("sfc", "lvl"), None), P(("sfc", "lvl")), P(), P(), P(), P(), P())
    lanes = mesh.shape["lvl"]
    n = mesh.shape["sfc"] * lanes
    return jax.shard_map(
        functools.partial(shards, n, lanes),
        mesh=mesh, in_specs=placed, out_specs=P(("sfc", "lvl"), None), check_vma=False,
    )
```

time: 98.9 us -> 40.4 us (0.41)
  the two profiles are of different devices: /device:TPU:6 before, /device:TPU:8 now
where the time goes in v1:
time: 40.4 us; the launch traced here: 40.2 us
  Pallas kernels  38.5 us (95%)
  local copies, waits for them, and re-layouts  1.67 us (4%)
    pallas_call x1, Pallas kernels, shards(): pl.pallas_call(functools.partial(cycle, n, lanes, cap), out_shape=jax.Sha...  38.5 us
    unnamed x1, local copies, waits for them, and re-layouts  1.67 us

profile of v1, /device:TPU:8, one launch (start us, length us, event | category | flops | bytes accessed | tf_op | source)
XLA Modules:
  0.0 40.2 jit_solution(8864469786954289996)
XLA Ops:
  0.0 38.5 %cycle.1 = f32[512,128]{1,0:T(8,128)} custom-call(s32[1024]{0:T(1024)} %counts_hbm.1, f32[512,128]{1,0:T(8,128)} %b_hbm.1, f32[4,128]{1,0:T(4,128)} %bitcast.1, f32[128,128]{1,0:T(8,128)} %cell_hbm.1, f32[128,128]{1,0:T(8,128)} %near_hbm.1, f32[128,128]{1,0:T(8,128)} %far_hbm.1, f32[8,128,128]{2,1,0:T(8,128)} %prolong_hbm.1), custom_call_target="tpu_custom_call" | custom-call | tf_op jit(solution)/shard_map/cycle/pallas_call | solution.py:379
  38.5 1.7 %copy.9 = f32[512,128]{1,0:T(8,128)} copy(f32[512,128]{1,0:T(8,128)} %cycle.1) | data formatting | bytes 524288

commit v2 on v1

--- a/solution.py
+++ b/solution.py
@@ -50,10 +50,11 @@
     main_w, low_w, rest_w, rest_low, pro_w, pro_low,
     c_own, c_tail, c_coef, l1, l2, l3, r1, r2, r3, k1, k2, k3, q1, q2, q3,
     c_b, c_a, c_j, c_x, c_d,
-    local_sem, b_send, b_recv, m_send, m_recv, c_send, c_recv,
+    x_tail, x_head, x_low, x_high,
+    local_sem, b_send, b_recv, m_send, m_recv, c_send, c_recv, x_send, x_recv,
 ):
     stride = cap // 16
-    depth = 5 * stride
+    depth = 3 * stride
     total = cap + 2 * depth
     c_cap = cap // 8
     base = c_cap + 16
@@ -69,10 +70,18 @@
         return (lax.div(t, lanes), lax.rem(t, lanes))
 
     barrier = pltpu.get_barrier_semaphore()
-    for s in STEPS:
-        pl.semaphore_signal(
-            barrier, inc=1, device_id=device(s), device_id_type=pl.DeviceIdType.MESH
-        )
+    def exists(step):
+        return me >= -step if step < 0 else me < n - step
+
+    def signal(step):
+        @pl.when(exists(step))
+        def _():
+            pl.semaphore_signal(
+                barrier, inc=1, device_id=device(step), device_id_type=pl.DeviceIdType.MESH
+            )
+
+    for step in STEPS:
+        signal(step)
     loads = [
         pltpu.make_async_copy(src, dst, local_sem.at[i])
         for i, (src, dst) in enumerate(
@@ -86,10 +95,26 @@
         c.start()
 
     def remote(src, dst, send, recv, slot):
-        return pltpu.make_async_remote_copy(
+        copy = pltpu.make_async_remote_copy(
             src_ref=src, dst_ref=dst, send_sem=send.at[slot], recv_sem=recv.at[slot],
             device_id=device(STEPS[slot]), device_id_type=pl.DeviceIdType.MESH,
         )
+        return copy, STEPS[slot]
+
+    def start(pair):
+        @pl.when(exists(pair[1]))
+        def _():
+            pair[0].start()
+
+    def received(pair):
+        @pl.when(exists(-pair[1]))
+        def _():
+            pair[0].wait_recv()
+
+    def sent(pair):
+        @pl.when(exists(pair[1]))
+        def _():
+            pair[0].wait_send()
 
     loads[0].wait()
     loads[1].wait()
@@ -113,7 +138,7 @@
 
     loads[2].wait()
     tail[...] = b_own[pl.ds(8 * (c_live - depth // 8), depth), :]
-    pl.semaphore_wait(barrier, len(STEPS))
+    pl.semaphore_wait(barrier, jnp.minimum(me, 3) + jnp.minimum(n - 1 - me, 3))
     halo = [
         remote(tail, ghost_low, b_send, b_recv, 0),
         remote(b_own.at[pl.ds(0, depth)], ghost_high.at[pl.ds(half, depth)], b_send, b_recv, 1),
@@ -121,12 +146,8 @@
     metas = [
         remote(meta, meta_in.at[i], m_send, m_recv, i) for i in range(len(STEPS))
     ]
-    metas[0].start()
-    metas[1].start()
-    for c in halo:
-        c.start()
-    for c in metas[2:]:
-        c.start()
+    for c in metas[:2] + halo + metas[2:]:
+        start(c)
 
     for c in loads[3:6]:
         c.wait()
@@ -157,21 +178,12 @@
     y[:, pl.ds(0, stride), :] = jnp.zeros((5, stride, 128), F32)
     y[:, pl.ds(stride + total, stride), :] = jnp.zeros((5, stride, 128), F32)
 
-    for c in metas:
-        c.wait_recv()
+    for c in metas[:2]:
+        received(c)
     for i in range(cap // 128):
         a_left[pl.ds(128 * i, 128), :] = columns(meta_in[0, pl.ds(i, 1), :])
     for i in range(2):
         a_high[pl.ds(half + 128 * i, 128), :] = columns(meta_in[1, pl.ds(i, 1), :])
-    for i, (ref, at_row, first, size) in enumerate(
-        [
-            (k1, 16, 128 - c_cap, c_cap), (q1, 32, 0, c_cap),
-            (k2, 0, 128 - 48, 48), (q2, 64, 0, 48),
-            (k3, 0, 128 - 16, 16), (q3, 96, 0, 16),
-        ]
-    ):
-        ref[pl.ds(at_row, size), :] = columns(meta_in[i, pl.ds(4, 1), :])[first : first + size]
-
     has_prev = me > 0
     has_next = me < n - 1
     left_live = count(at(-1))
@@ -194,7 +206,7 @@
     wide_j[...] = jnp.where(is_live, 1.0 / (jnp.where(is_live, wide_a[...], 16.0) + diag), 0.0)
 
     for c in halo:
-        c.wait_recv()
+        received(c)
     wide_b[pl.ds(0, depth), :] = jnp.where(
         rows_of(0, depth) >= low_limit, ghost_low[...], 0.0
     )
@@ -266,6 +278,12 @@
         acc = acc + jnp.dot(hi, rest_low[pl.ds(128 * i, 128), :], preferred_element_type=F32)
     c_own[pl.ds(c_cap, c_cap), :] = acc
     c_tail[...] = c_own[pl.ds(c_live, c_cap), :]
+    x_tail[...] = x[pl.ds(8 * c_live, depth), :]
+    x_head[...] = x[pl.ds(depth, depth), :]
+    halo_x = [
+        remote(x_tail, x_low, x_send, x_recv, 0),
+        remote(x_head, x_high.at[pl.ds(half, depth)], x_send, x_recv, 1),
+    ]
     coarse = [
         remote(c_tail, l1.at[pl.ds(16, c_cap)], c_send, c_recv, 0),
         remote(c_own.at[pl.ds(c_cap, c_cap)], r1.at[pl.ds(32, c_cap)], c_send, c_recv, 1),
@@ -274,8 +292,19 @@
         remote(c_tail.at[pl.ds(c_cap - 16, 16)], l3.at[pl.ds(0, 16)], c_send, c_recv, 4),
         remote(c_own.at[pl.ds(c_cap, 16)], r3.at[pl.ds(96, 16)], c_send, c_recv, 5),
     ]
-    for c in coarse:
-        c.start()
+    for c in coarse + halo_x:
+        start(c)
+    for c in metas[2:]:
+        received(c)
+    for i, (ref, at_row, first, size) in enumerate(
+        [
+            (k1, 16, 128 - c_cap, c_cap), (q1, 32, 0, c_cap),
+            (k2, 0, 128 - 48, 48), (q2, 64, 0, 48),
+            (k3, 0, 128 - 16, 16), (q3, 96, 0, 16),
+        ]
+    ):
+        ref[pl.ds(at_row, size), :] = columns(meta_in[i, pl.ds(4, 1), :])[first : first + size]
+
 
     n2 = lax.div(count(at(-2)), 8)
     p1 = lax.div(count(at(1)), 8)
@@ -315,7 +344,7 @@
         c_live_rows, 1.0 / (jnp.where(c_live_rows, c_a[...], 16.0) + diag), 0.0
     )
     for c in coarse:
-        c.wait_recv()
+        received(c)
     gathered(c_b, acc, l1, l2, l3, r1, r2, r3)
     first = c_j[...] * c_b[...] * (1.0 / CENTER)
     c_x[...] = first
@@ -324,31 +353,41 @@
         low = stride * (i + 1)
         improve(c_x, c_d, c_a, c_j, c_b, low, c_total - low, keep, gain)
 
-    rows = c_cap + 32
-    hi, lo = split(c_x[pl.ds(base - 16, rows), :])
+    for c in halo_x:
+        received(c)
+    x[pl.ds(0, depth), :] = jnp.where(rows_of(0, depth) >= low_limit, x_low[...], 0.0)
+    more_x = x_high[pl.ds(shift, cap + depth - half), :]
+    x[pl.ds(depth + half, cap + depth - half), :] = jnp.where(
+        inside,
+        x[pl.ds(depth + half, cap + depth - half), :],
+        jnp.where(index < high_limit, more_x, 0.0),
+    )
+    edge = depth // 8
+    rows = c_cap + 2 * edge
+    hi, lo = split(c_x[pl.ds(base - edge, rows), :])
     pair = jnp.concatenate([hi, lo], 1)
     for start in range(0, 1024, 256):
         part = jnp.dot(
             pair, pro_w[:, pl.ds(start, 256)], preferred_element_type=F32
         ) + jnp.dot(hi, pro_low[:, pl.ds(start, 256)], preferred_element_type=F32)
         for k in range(2):
-            where = pl.ds(depth - 128 + start // 128 + k, rows, stride=8)
+            where = pl.ds(start // 128 + k, rows, stride=8)
             x[where, :] = x[where, :] + part[:, 128 * k : 128 * k + 128]
 
-    low, high = depth - 2 * stride, depth + cap + 2 * stride
+    low, high = stride, total - stride
     improve(x, d, wide_a, wide_j, wide_b, low, high, None, 1.0 / CENTER)
     for keep, gain in pairs:
         low, high = low + stride, high - stride
         improve(x, d, wide_a, wide_j, wide_b, low, high, keep, gain)
     out_ref[...] = jnp.where(rows_of(0, cap) < live, x[pl.ds(depth, cap), :], 0.0)
-    for c in halo + metas + coarse:
-        c.wait_send()
+    for c in halo + metas + coarse + halo_x:
+        sent(c)
 
 
 def shards(n, lanes, right_side, cell_coef, fine_count, cell_matrix, face_near, face_far, prolong):
     cap = right_side.shape[0]
     stride = cap // 16
-    depth = 5 * stride
+    depth = 3 * stride
     total = cap + 2 * depth
     c_cap = cap // 8
     base = c_cap + 16
@@ -374,19 +413,27 @@
     for _ in range(2):
         scratch += [vmem(base, 128)] * 3 + [vmem(base + c_cap, 128)] * 3
     scratch += [vmem(c_total, 128)] * 5
+    scratch += [vmem(depth, 128), vmem(depth, 128), vmem(depth, 128), vmem(cap + depth, 128)]
     dma = pltpu.SemaphoreType.DMA
-    scratch += [dma((7,)), dma((2,)), dma((2,)), dma((6,)), dma((6,)), dma((6,)), dma((6,))]
+    scratch += [dma((7,)), dma((2,)), dma((2,)), dma((6,)), dma((6,)), dma((6,)), dma((6,)), dma((2,)), dma((2,))]
     return pl.pallas_call(
         functools.partial(cycle, n, lanes, cap),
         out_shape=jax.ShapeDtypeStruct(right_side.shape, F32),
-        in_specs=[pl.BlockSpec(memory_space=pl.ANY)] * 7,
+        in_specs=[pl.BlockSpec(memory_space=pltpu.MemorySpace.HBM)] * 7,
         out_specs=pl.BlockSpec(memory_space=pltpu.VMEM),
         scratch_shapes=scratch,
-        compiler_params=pltpu.CompilerParams(collective_id=0, has_side_effects=True),
+        compiler_params=pltpu.CompilerParams(
+            collective_id=0, has_side_effects=True, vmem_limit_bytes=32 * 2**20
+        ),
         name="cycle",
     )(
-        fine_count, right_side, cell_coef.reshape(4, 128), cell_matrix, face_near, face_far,
-        prolong,
+        *(
+            pltpu.with_memory_space_constraint(v, pltpu.MemorySpace.HBM)
+            for v in (
+                fine_count, right_side, cell_coef.reshape(4, 128), cell_matrix, face_near,
+                face_far, prolong,
+            )
+        )
     )
 
 

time: 40.4 us -> 35.8 us (0.89)
  the two profiles are of different devices: /device:TPU:8 before, /device:TPU:6 now
where the time goes in v2:
time: 35.8 us; the launch traced here: 35.7 us
  Pallas kernels  35 us (98%)
  local copies, waits for them, and re-layouts  0.71 us (2%)
    pallas_call x1, Pallas kernels, shards(): pl.pallas_call(functools.partial(cycle, n, lanes, cap), out_shape=jax.Sha...  35 us

profile of v2, /device:TPU:6, one launch (start us, length us, event | category | flops | bytes accessed | tf_op | source)
XLA Modules:
  0.0 35.7 jit_solution(12423188263013096363)
XLA Ops:
  0.0 35.0 %cycle.1 = f32[512,128]{1,0:T(8,128)S(1)} custom-call(s32[1024]{0:T(1024)} %counts_hbm.1, f32[512,128]{1,0:T(8,128)} %b_hbm.1, f32[4,128]{1,0:T(4,128)} %bitcast.1, f32[128,128]{1,0:T(8,128)} %cell_hbm.1, f32[128,128]{1,0:T(8,128)} %near_hbm.1, f32[128,128]{1,0:T(8,128)} %far_hbm.1, f32[8,128,128]{2,1,0:T(8,128)} %prolong_hbm.1), custom_call_target="tpu_custom_call" | custom-call | tf_op jit(solution)/shard_map/cycle/pallas_call | solution.py:419
  35.0 0.7 %copy.9 = f32[512,128]{1,0:T(8,128)} copy(f32[512,128]{1,0:T(8,128)S(1)} %cycle.1) | data formatting | bytes 524288

commit v3 on v2

v3 whole, which is shorter than its diff:
```python
import functools

import jax
import jax.numpy as jnp
from jax import lax
from jax.experimental import pallas as pl
from jax.experimental.pallas import tpu as pltpu
from jax.sharding import PartitionSpec as P

DEG = 3
CENTER = 1.025
RADIUS = 0.775
STEPS = (1, -1, 2, -2, 3, -3)
F32 = jnp.float32
BF16 = jnp.bfloat16


def weights_of():
    ratio = CENTER / RADIUS
    prev = 1.0 / ratio
    pairs = []
    for _ in range(DEG - 1):
        new = 1.0 / (2.0 * ratio - prev)
        pairs.append((new * prev, 2.0 * new / RADIUS))
        prev = new
    return pairs


def split(x):
    high = x.astype(BF16)
    low = (x - high.astype(F32)).astype(BF16)
    return high, low


def rows_of(start, size):
    return start + lax.broadcasted_iota(jnp.int32, (size, 128), 0)


def columns(row):
    return jnp.transpose(jnp.broadcast_to(row, (128, 128)))


def cycle(
    n, lanes, cap,
    counts_hbm, b_hbm, coef_hbm, cell_hbm, near_hbm, far_hbm, prolong_hbm,
    out_ref,
    counts, b_own, coef, cell, near, far, prolong,
    tail, ghost_low, ghost_high, meta, meta_in,
    a_left, a_high, wide_b, wide_a, wide_j, x, d, y, res,
    strip1, strip2, strip3, strip_d,
    main_w, mix_w, rest_w, pro_w, pro_low,
    c_own, c_tail, c_coef, l1, l2, r1, r2, r3, k1, k2, k3, q1, q2, q3,
    c_b, c_a, c_j, c_x, c_d, x_head, x_high,
    local_sem, b_send, b_recv, m_send, m_recv, c_send, c_recv, x_send, x_recv,
):
    stride = cap // 16
    left = 6 * stride
    right = 3 * stride
    total = left + cap + right
    inner = left + cap
    c_cap = cap // 8
    edge = right // 8
    base = c_cap + 16
    c_total = base + c_cap + base
    half = cap // 2
    more = half + right
    me = lax.axis_index("sfc") * lanes + lax.axis_index("lvl")

    def at(step):
        return lax.rem(me + (step + n), n)

    def device(step):
        t = at(step)
        return (lax.div(t, lanes), lax.rem(t, lanes))

    def exists(step):
        return me >= -step if step < 0 else me < n - step

    barrier = pltpu.get_barrier_semaphore()

    def signal(step):
        @pl.when(exists(step))
        def _():
            pl.semaphore_signal(
                barrier, inc=1, device_id=device(step), device_id_type=pl.DeviceIdType.MESH
            )

    for step in STEPS:
        signal(step)
    loads = [
        pltpu.make_async_copy(src, dst, local_sem.at[i])
        for i, (src, dst) in enumerate(
            [
                (counts_hbm, counts), (coef_hbm, coef), (b_hbm, b_own), (cell_hbm, cell),
                (near_hbm, near), (far_hbm, far), (prolong_hbm, prolong),
            ]
        )
    ]
    for c in loads:
        c.start()

    def remote(src, dst, send, recv, slot, sem=None):
        sem = slot if sem is None else sem
        copy = pltpu.make_async_remote_copy(
            src_ref=src, dst_ref=dst, send_sem=send.at[sem], recv_sem=recv.at[sem],
            device_id=device(STEPS[slot]), device_id_type=pl.DeviceIdType.MESH,
        )
        return copy, STEPS[slot]

    def start(pair):
        @pl.when(exists(pair[1]))
        def _():
            pair[0].start()

    def received(pair):
        @pl.when(exists(-pair[1]))
        def _():
            pair[0].wait_recv()

    def sent(pair):
        @pl.when(exists(pair[1]))
        def _():
            pair[0].wait_send()

    loads[0].wait()
    loads[1].wait()

    def count(t):
        return jnp.minimum(jnp.maximum(counts[t], half), cap)

    live = count(me)
    c_live = lax.div(live, 8)
    for i in range(cap // 128):
        wide_a[pl.ds(left + 128 * i, 128), :] = columns(coef[pl.ds(i, 1), :])
    mean = wide_a[pl.ds(left, c_cap, stride=8), :]
    for c in range(1, 8):
        mean = mean + wide_a[pl.ds(left + c, c_cap, stride=8), :]
    mean = mean * 0.125
    c_coef[pl.ds(0, c_cap), :] = jnp.zeros((c_cap, 128), F32)
    c_coef[pl.ds(c_cap, c_cap), :] = mean
    both = jnp.concatenate([mean, c_coef[pl.ds(c_live, c_cap), :]], 0)
    meta[pl.ds(0, 4), :] = coef[...]
    meta[pl.ds(4, 4), :] = jnp.transpose(both)[0:4, :]

    loads[2].wait()
    tail[...] = b_own[pl.ds(8 * (c_live - left // 8), left), :]
    pl.semaphore_wait(barrier, jnp.minimum(me, 3) + jnp.minimum(n - 1 - me, 3))
    halo = [
        remote(tail, ghost_low, b_send, b_recv, 0),
        remote(b_own.at[pl.ds(0, right)], ghost_high.at[pl.ds(half, right)], b_send, b_recv, 1),
    ]
    metas = [
        remote(meta, meta_in.at[i], m_send, m_recv, i) for i in range(len(STEPS))
    ]
    for c in [metas[0], halo[0], metas[1], halo[1]] + metas[2:]:
        start(c)

    for c in loads[3:6]:
        c.wait()
    cell_m = cell[...]
    parts = [cell_m, -near[...], -jnp.transpose(near[...]), -far[...], -jnp.transpose(far[...])]
    parts = [split(m) for m in parts]
    (c_hi, c_lo), (n_hi, n_lo), (nt_hi, nt_lo), (f_hi, f_lo), (ft_hi, ft_lo) = parts
    for i, (upper, lower) in enumerate(
        [
            (n_hi, n_hi), (ft_hi, ft_hi), (nt_hi, nt_hi), (f_hi, f_hi), (c_hi, c_hi),
            (c_lo, jnp.zeros_like(c_lo)),
        ]
    ):
        main_w[pl.ds(0, 128), pl.ds(128 * i, 128)] = upper
        main_w[pl.ds(128, 128), pl.ds(128 * i, 128)] = lower
    for i, (upper, lower) in enumerate([(n_lo, f_lo), (ft_lo, nt_lo)]):
        mix_w[pl.ds(0, 128), pl.ds(128 * i, 128)] = upper
        mix_w[pl.ds(128, 128), pl.ds(128 * i, 128)] = lower
    eye = lax.broadcasted_iota(jnp.int32, (128, 128), 0) == lax.broadcasted_iota(
        jnp.int32, (128, 128), 1
    )
    diag = jnp.sum(jnp.where(eye, cell_m, 0.0), axis=0, keepdims=True)
    y[:, pl.ds(0, stride), :] = jnp.zeros((5, stride, 128), F32)
    y[:, pl.ds(stride + total, stride), :] = jnp.zeros((5, stride, 128), F32)
    for ref in (strip1, strip2, strip3):
        ref[pl.ds(8 * stride, stride), :] = jnp.zeros((stride, 128), F32)
    c_x[pl.ds(c_total, stride), :] = jnp.zeros((stride, 128), F32)
    x[pl.ds(inner, right + stride), :] = jnp.zeros((right + stride, 128), F32)
    wide_a[pl.ds(inner, right), :] = jnp.zeros((right, 128), F32)
    c_own[...] = jnp.zeros_like(c_own)
    res[pl.ds(right + cap, stride), :] = jnp.zeros((stride, 128), F32)

    def products(field, first, size):
        hi, lo = split(field[pl.ds(first, size), :])
        pair = jnp.concatenate([hi, lo], 1)
        ahead = field[pl.ds(first + stride - 1, size), :].astype(BF16)
        rows = pl.ds(stride + first, size)
        part = jnp.dot(
            pair, main_w[:, pl.ds(0, 256)], preferred_element_type=F32
        ) + jnp.dot(
            jnp.concatenate([hi, ahead], 1), mix_w[...], preferred_element_type=F32
        )
        y[1, rows, :] = part[:, :128]
        y[4, rows, :] = part[:, 128:]
        part = jnp.dot(pair, main_w[:, pl.ds(256, 256)], preferred_element_type=F32)
        y[2, rows, :] = part[:, :128]
        y[3, rows, :] = part[:, 128:]
        part = jnp.dot(pair, main_w[:, pl.ds(512, 256)], preferred_element_type=F32)
        y[0, rows, :] = part[:, :128] + part[:, 128:]

    def residual(field, coefs, source, low, high, shift=0):
        size = high - low
        products(field, low - stride, size + 2 * stride)
        row = stride + low
        wide = pl.ds(low + shift, size)
        return source[wide, :] - (
            coefs[wide, :] * field[pl.ds(low, size), :]
            + y[0, pl.ds(row, size), :]
            + y[1, pl.ds(row + 1, size), :]
            + y[2, pl.ds(row - 1, size), :]
            + y[3, pl.ds(row + stride, size), :]
            + y[4, pl.ds(row - stride, size), :]
        )

    def improve(field, update, coefs, scale, source, low, high, keep, gain):
        rows = pl.ds(low, high - low)
        step = gain * scale[rows, :] * residual(field, coefs, source, low, high)
        if keep is not None:
            step = keep * update[rows, :] + step
        update[rows, :] = step
        field[rows, :] = field[rows, :] + step

    pairs = weights_of()
    has_prev = me > 0
    has_next = me < n - 1

    own = pl.ds(left, cap)
    own_rows = rows_of(0, cap) < live
    own_j = jnp.where(own_rows, 1.0 / (wide_a[own, :] + diag), 0.0)
    own_b = jnp.where(own_rows, b_own[...], 0.0)
    wide_j[own, :] = own_j
    wide_b[own, :] = own_b
    wide_j[pl.ds(inner, right), :] = jnp.zeros((right, 128), F32)
    wide_b[pl.ds(inner, right), :] = jnp.zeros((right, 128), F32)
    first = own_j * own_b * (1.0 / CENTER)
    x[own, :] = first
    d[own, :] = first
    strip1[pl.ds(left, 2 * stride), :] = first[: 2 * stride]
    improve(x, d, wide_a, wide_j, wide_b, left + stride, inner, *pairs[0])
    strip2[pl.ds(left, 2 * stride), :] = x[pl.ds(left + stride, 2 * stride), :]
    strip_d[pl.ds(left, 2 * stride), :] = d[pl.ds(left + stride, 2 * stride), :]
    improve(x, d, wide_a, wide_j, wide_b, left + 2 * stride, inner, *pairs[1])
    strip3[pl.ds(left, 2 * stride), :] = x[pl.ds(left + 2 * stride, 2 * stride), :]
    res[pl.ds(2 * right, cap - right), :] = residual(
        x, wide_a, wide_b, left + right, inner
    )

    loads[6].wait()
    for i in range(8):
        m = prolong[i]
        high, low = split(m)
        pro_w[pl.ds(0, 128), pl.ds(128 * i, 128)] = high
        pro_w[pl.ds(128, 128), pl.ds(128 * i, 128)] = high
        pro_low[:, pl.ds(128 * i, 128)] = low
        high, low = split(jnp.transpose(m))
        for k in range(2):
            rest_w[pl.ds(256 * i + 128 * k, 128), pl.ds(0, 128)] = high
            rest_w[pl.ds(256 * i + 128 * k, 128), pl.ds(128, 128)] = low

    low_limit = jnp.where(has_prev, 0, left)
    left_rows = rows_of(0, left) >= low_limit
    received(metas[0])
    for i in range(cap // 128):
        a_left[pl.ds(128 * i, 128), :] = columns(meta_in[0, pl.ds(i, 1), :])
    n1 = lax.div(count(at(-1)), 8)
    a_low = jnp.where(left_rows, a_left[pl.ds(8 * (n1 - left // 8), left), :], 0.0)
    wide_a[pl.ds(0, left), :] = a_low
    j_low = jnp.where(left_rows, 1.0 / (jnp.where(left_rows, a_low, 16.0) + diag), 0.0)
    wide_j[pl.ds(0, left), :] = j_low

    received(halo[0])
    b_low = jnp.where(left_rows, ghost_low[...], 0.0)
    wide_b[pl.ds(0, left), :] = b_low
    strip1[pl.ds(0, left), :] = j_low * b_low * (1.0 / CENTER)
    low, high = stride, 7 * stride
    middle = pl.ds(low, high - low)
    keep, gain = pairs[0]
    step = gain * wide_j[middle, :] * residual(strip1, wide_a, wide_b, low, high)
    step = keep * strip1[middle, :] + step
    strip_d[pl.ds(0, left), :] = step
    strip2[pl.ds(0, left), :] = strip1[middle, :] + step
    keep, gain = pairs[1]
    step = gain * wide_j[pl.ds(low + stride, left), :] * residual(
        strip2, wide_a, wide_b, low, high, stride
    )
    step = keep * strip_d[middle, :] + step
    strip3[pl.ds(0, left), :] = strip2[middle, :] + step
    res[pl.ds(0, left), :] = residual(strip3, wide_a, wide_b, low, high, 2 * stride)

    acc = jnp.zeros((base, 256), F32)
    for i in range(8):
        hi, lo = split(res[pl.ds(i, base, stride=8), :])
        acc = acc + jnp.dot(
            jnp.concatenate([hi, lo], 1), rest_w[pl.ds(256 * i, 256), :],
            preferred_element_type=F32,
        )
    front = c_cap + 8
    c_own[pl.ds(front, base), :] = acc[:, :128] + acc[:, 128:]
    c_tail[...] = c_own[pl.ds(8 + c_live, c_cap), :]
    coarse = [
        remote(c_tail, l1.at[pl.ds(8, c_cap)], c_send, c_recv, 0),
        remote(c_own.at[pl.ds(front, base)], r1.at[pl.ds(40, base)], c_send, c_recv, 1),
        remote(c_tail.at[pl.ds(c_cap - 32, 32)], l2.at[pl.ds(8, 32)], c_send, c_recv, 2),
        remote(c_own.at[pl.ds(front, 56)], r2.at[pl.ds(72, 56)], c_send, c_recv, 3),
        remote(c_own.at[pl.ds(front, 24)], r3.at[pl.ds(104, 24)], c_send, c_recv, 5, 4),
    ]
    for c in coarse:
        start(c)
    x[pl.ds(2 * stride, left), :] = strip3[pl.ds(0, left), :]
    x_head[...] = x[pl.ds(left - 2 * stride, 5 * stride), :]
    halo_x = remote(x_head, x_high.at[pl.ds(half, 5 * stride)], x_send, x_recv, 1, 0)
    start(halo_x)

    for c in metas[1:]:
        received(c)
    for i in range(2):
        a_high[pl.ds(half + 128 * i, 128), :] = columns(meta_in[1, pl.ds(i, 1), :])
    for i, (ref, at_row, top, size) in enumerate(
        [
            (k1, 16, 128 - c_cap, c_cap), (q1, 32, 0, c_cap),
            (k2, 0, 128 - 48, 48), (q2, 64, 0, 48),
            (k3, 0, 128 - 16, 16), (q3, 96, 0, 16),
        ]
    ):
        ref[pl.ds(at_row, size), :] = columns(meta_in[i, pl.ds(4, 1), :])[top : top + size]
    received(halo[1])
    shift = 8 * (cap // 8 - c_live)
    index = rows_of(half, more)
    limit = live + jnp.where(has_next, right, 0)
    late = pl.ds(left + half, more)
    old = index < live
    new = index < limit
    late_a = jnp.where(
        new, jnp.where(old, wide_a[late, :], a_high[pl.ds(shift, more), :]), 0.0
    )
    wide_a[late, :] = late_a
    wide_j[late, :] = jnp.where(new, 1.0 / (jnp.where(new, late_a, 16.0) + diag), 0.0)
    wide_b[late, :] = jnp.where(
        new, jnp.where(old, wide_b[late, :], ghost_high[pl.ds(shift, more), :]), 0.0
    )

    n2 = lax.div(count(at(-2)), 8)
    p1 = lax.div(count(at(1)), 8)
    p2 = lax.div(count(at(2)), 8)
    e2 = base - n1
    e3 = e2 - n2
    s1 = base + c_live
    s2 = s1 + p1
    s3 = s2 + p2
    reach = c_cap + edge
    c_low = jnp.maximum(
        base - reach, jnp.where(me >= 3, 0, jnp.where(me == 2, e3, jnp.where(me == 1, e2, base)))
    )
    c_high = jnp.minimum(
        s1 + reach,
        jnp.where(
            me + 3 < n, s3 + reach,
            jnp.where(me + 3 == n, s3, jnp.where(me + 2 == n, s2, s1)),
        ),
    )

    def zeros(rows):
        return jnp.zeros((rows, 128), F32)

    r = rows_of(0, base)
    v2 = jnp.concatenate([k2[pl.ds(48 - e2, 48), :], zeros(base - 48)], 0)
    v3 = jnp.concatenate([k3[pl.ds(16 - e3, 16), :], zeros(base - 16)], 0)
    value = jnp.where(r >= e2, k1[...], jnp.where(r >= e3, v2, v3))
    c_a[pl.ds(0, base), :] = jnp.where(r >= c_low, value, 0.0)
    r = rows_of(base, c_cap + base)
    v0 = jnp.concatenate([mean, zeros(base)], 0)
    v1 = jnp.concatenate([zeros(32), q1[pl.ds(c_cap - c_live, 112), :]], 0)
    v2 = jnp.concatenate([zeros(64), q2[pl.ds(208 - s2, 80), :]], 0)
    v3 = jnp.concatenate([zeros(96), q3[pl.ds(272 - s3, 48), :]], 0)
    value = jnp.where(r < s1, v0, jnp.where(r < s2, v1, jnp.where(r < s3, v2, v3)))
    c_a[pl.ds(base, c_cap + base), :] = jnp.where(r < c_high, value, 0.0)
    r = rows_of(0, c_total)
    c_live_rows = (r >= c_low) & (r < c_high)
    c_j[...] = jnp.where(
        c_live_rows, 1.0 / (jnp.where(c_live_rows, c_a[...], 16.0) + diag), 0.0
    )

    for c in coarse:
        received(c)
    o1 = s1 - edge
    o2 = s2 - edge
    o3 = s3 - edge
    t1 = jnp.where(me == n - 1, c_total, o1)
    t2 = jnp.where(me == n - 2, c_total, o2)
    t3 = jnp.where(me == n - 3, c_total, o3)
    f2 = e2 - edge
    r = rows_of(0, front)
    v1 = l1[pl.ds(4, front), :]
    v2 = jnp.concatenate([l2[pl.ds(40 - f2, 40), :], zeros(front - 40)], 0)
    value = jnp.where(
        r >= base - edge, c_own[pl.ds(4, front), :], jnp.where(r >= f2, v1, v2)
    )
    c_b[pl.ds(0, front), :] = jnp.where(r >= c_low, value, 0.0)
    r = rows_of(front, c_total - front)
    v0 = jnp.concatenate([c_own[pl.ds(front + 4, base), :], zeros(front)], 0)
    v1 = jnp.concatenate([zeros(24), r1[pl.ds(136 - o1, 128), :]], 0)
    v2 = jnp.concatenate([zeros(56), r2[pl.ds(200 - o2, 96), :]], 0)
    v3 = jnp.concatenate([zeros(88), r3[pl.ds(264 - o3, 64), :]], 0)
    value = jnp.where(r < t1, v0, jnp.where(r < t2, v1, jnp.where(r < t3, v2, v3)))
    c_b[pl.ds(front, c_total - front), :] = jnp.where(
        (r >= c_low) & (r < c_high), value, 0.0
    )
    first = c_j[...] * c_b[...] * (1.0 / CENTER)
    c_x[pl.ds(0, c_total), :] = first
    c_d[...] = first
    for i, (keep, gain) in enumerate(pairs):
        low = stride * (i + 1)
        improve(c_x, c_d, c_a, c_j, c_b, low, c_total - low, keep, gain)

    received(halo_x)
    index = rows_of(left, cap + right - left)
    keep_x = live - jnp.where(has_next, 2 * stride, 0)
    late = pl.ds(2 * left, cap + right - left)
    x[late, :] = jnp.where(
        index < limit,
        jnp.where(index < keep_x, x[late, :], x_high[pl.ds(shift, cap + right - left), :]),
        0.0,
    )
    rows = c_cap + 2 * edge
    hi, lo = split(c_x[pl.ds(base - edge, rows), :])
    pair = jnp.concatenate([hi, lo], 1)
    for begin in range(0, 1024, 256):
        part = jnp.dot(
            pair, pro_w[:, pl.ds(begin, 256)], preferred_element_type=F32
        ) + jnp.dot(hi, pro_low[:, pl.ds(begin, 256)], preferred_element_type=F32)
        for k in range(2):
            where = pl.ds(right + begin // 128 + k, rows, stride=8)
            x[where, :] = x[where, :] + part[:, 128 * k : 128 * k + 128]

    low, high = left - 2 * stride, total - stride
    improve(x, d, wide_a, wide_j, wide_b, low, high, None, 1.0 / CENTER)
    for keep, gain in pairs:
        low, high = low + stride, high - stride
        improve(x, d, wide_a, wide_j, wide_b, low, high, keep, gain)
    out_ref[...] = jnp.where(own_rows, x[own, :], 0.0)
    for c in halo + metas + coarse + [halo_x]:
        sent(c)


def shards(n, lanes, right_side, cell_coef, fine_count, cell_matrix, face_near, face_far, prolong):
    cap = right_side.shape[0]
    stride = cap // 16
    left = 6 * stride
    right = 3 * stride
    total = left + cap + right
    c_cap = cap // 8
    base = c_cap + 16
    c_total = 2 * base + c_cap
    half = cap // 2

    def vmem(*shape, dtype=F32):
        return pltpu.VMEM(shape, dtype)

    scratch = [
        pltpu.SMEM(fine_count.shape, jnp.int32), vmem(cap, 128), vmem(4, 128),
        vmem(128, 128), vmem(128, 128), vmem(128, 128), vmem(8, 128, 128),
        vmem(left, 128), vmem(left, 128), vmem(cap + right, 128), vmem(8, 128),
        vmem(6, 8, 128),
        vmem(cap, 128), vmem(cap + right, 128), vmem(total, 128), vmem(total, 128),
        vmem(total, 128), vmem(total + stride, 128), vmem(total, 128),
        vmem(5, total + 2 * stride, 128), vmem(cap + right + stride, 128),
        vmem(9 * stride, 128), vmem(9 * stride, 128), vmem(9 * stride, 128),
        vmem(8 * stride, 128),
        vmem(256, 768, dtype=BF16), vmem(256, 256, dtype=BF16),
        vmem(2048, 256, dtype=BF16),
        vmem(256, 1024, dtype=BF16), vmem(128, 1024, dtype=BF16),
        vmem(160, 128), vmem(c_cap, 128), vmem(2 * c_cap, 128),
        vmem(88, 128), vmem(80, 128), vmem(168, 128), vmem(168, 128), vmem(168, 128),
    ]
    scratch += [vmem(base, 128)] * 3 + [vmem(base + c_cap, 128)] * 3
    scratch += [vmem(c_total, 128)] * 3 + [vmem(c_total + stride, 128), vmem(c_total, 128)]
    scratch += [vmem(5 * stride, 128), vmem(half + 416, 128)]
    dma = pltpu.SemaphoreType.DMA
    scratch += [dma((7,)), dma((2,)), dma((2,)), dma((6,)), dma((6,)), dma((5,)), dma((5,))]
    scratch += [dma((1,)), dma((1,))]
    return pl.pallas_call(
        functools.partial(cycle, n, lanes, cap),
        out_shape=jax.ShapeDtypeStruct(right_side.shape, F32),
        in_specs=[pl.BlockSpec(memory_space=pltpu.MemorySpace.HBM)] * 7,
        out_specs=pl.BlockSpec(memory_space=pltpu.VMEM),
        scratch_shapes=scratch,
        compiler_params=pltpu.CompilerParams(
            collective_id=0, has_side_effects=True, vmem_limit_bytes=32 * 2**20
        ),
        name="cycle",
    )(
        *(
            pltpu.with_memory_space_constraint(v, pltpu.MemorySpace.HBM)
            for v in (
                fine_count, right_side, cell_coef.reshape(4, 128), cell_matrix, face_near,
                face_far, prolong,
            )
        )
    )


def solution(mesh):
    placed = (P(("sfc", "lvl"), None), P(("sfc", "lvl")), P(), P(), P(), P(), P())
    lanes = mesh.shape["lvl"]
    n = mesh.shape["sfc"] * lanes
    return jax.shard_map(
        functools.partial(shards, n, lanes),
        mesh=mesh, in_specs=placed, out_specs=P(("sfc", "lvl"), None), check_vma=False,
    )
```

time: 35.8 us -> 32.4 us (0.905)
  Pallas kernels: 35 us -> 31.5 us
    pallas_call x1, Pallas kernels: 35 us -> 31.5 us  [shards(): pl.pallas_call(functools.partial(cycle, n, lanes, cap), out_shape=jax.Sha...]
where the time goes in v3:
time: 32.4 us; the launch traced here: 32.2 us
  Pallas kernels  31.5 us (97%)
  local copies, waits for them, and re-layouts  0.71 us (2%)
    pallas_call x1, Pallas kernels, shards(): pl.pallas_call(functools.partial(cycle, n, lanes, cap), out_shape=jax.Sha...  31.5 us
    unnamed x1, local copies, waits for them, and re-layouts  0.71 us

profile of v3, /device:TPU:6, one launch (start us, length us, event | category | flops | bytes accessed | tf_op | source)
XLA Modules:
  0.0 32.2 jit_solution(2852934695261728348)
XLA Ops:
  0.0 31.5 %cycle.1 = f32[512,128]{1,0:T(8,128)S(1)} custom-call(s32[1024]{0:T(1024)} %counts_hbm.1, f32[512,128]{1,0:T(8,128)} %b_hbm.1, f32[4,128]{1,0:T(4,128)} %bitcast.1, f32[128,128]{1,0:T(8,128)} %cell_hbm.1, f32[128,128]{1,0:T(8,128)} %near_hbm.1, f32[128,128]{1,0:T(8,128)} %far_hbm.1, f32[8,128,128]{2,1,0:T(8,128)} %prolong_hbm.1), custom_call_target="tpu_custom_call" | custom-call | tf_op jit(solution)/shard_map/cycle/pallas_call | solution.py:487
  31.5 0.7 %copy.9 = f32[512,128]{1,0:T(8,128)} copy(f32[512,128]{1,0:T(8,128)S(1)} %cycle.1) | data formatting | bytes 524288

commit v4 on v3

--- a/solution.py
+++ b/solution.py
@@ -85,7 +85,7 @@
                 barrier, inc=1, device_id=device(step), device_id_type=pl.DeviceIdType.MESH
             )
 
-    for step in STEPS:
+    for step in (-1, -2, -3):
         signal(step)
     loads = [
         pltpu.make_async_copy(src, dst, local_sem.at[i])
@@ -144,7 +144,11 @@
 
     loads[2].wait()
     tail[...] = b_own[pl.ds(8 * (c_live - left // 8), left), :]
-    pl.semaphore_wait(barrier, jnp.minimum(me, 3) + jnp.minimum(n - 1 - me, 3))
+
+    @pl.when(me < n - 1)
+    def _():
+        pl.semaphore_wait(barrier, jnp.minimum(n - 1 - me, 3))
+
     halo = [
         remote(tail, ghost_low, b_send, b_recv, 0),
         remote(b_own.at[pl.ds(0, right)], ghost_high.at[pl.ds(half, right)], b_send, b_recv, 1),
@@ -152,8 +156,15 @@
     metas = [
         remote(meta, meta_in.at[i], m_send, m_recv, i) for i in range(len(STEPS))
     ]
-    for c in [metas[0], halo[0], metas[1], halo[1]] + metas[2:]:
-        start(c)
+    early = lax.rem(lax.axis_index("sfc"), 2) == 1
+    start(metas[0])
+
+    @pl.when(early)
+    def _():
+        start(halo[0])
+
+    start(metas[2])
+    start(metas[4])
 
     for c in loads[3:6]:
         c.wait()
@@ -251,6 +262,10 @@
         x, wide_a, wide_b, left + right, inner
     )
 
+    @pl.when(jnp.logical_not(early))
+    def _():
+        start(halo[0])
+
     loads[6].wait()
     for i in range(8):
         m = prolong[i]
@@ -266,6 +281,11 @@
     low_limit = jnp.where(has_prev, 0, left)
     left_rows = rows_of(0, left) >= low_limit
     received(metas[0])
+    start(metas[1])
+    start(halo[1])
+    for c, other in ((metas[2], metas[3]), (metas[4], metas[5])):
+        received(c)
+        start(other)
     for i in range(cap // 128):
         a_left[pl.ds(128 * i, 128), :] = columns(meta_in[0, pl.ds(i, 1), :])
     n1 = lax.div(count(at(-1)), 8)
@@ -317,7 +337,7 @@
     halo_x = remote(x_head, x_high.at[pl.ds(half, 5 * stride)], x_send, x_recv, 1, 0)
     start(halo_x)
 
-    for c in metas[1:]:
+    for c in metas[1::2]:
         received(c)
     for i in range(2):
         a_high[pl.ds(half + 128 * i, 128), :] = columns(meta_in[1, pl.ds(i, 1), :])

time: 32.4 us -> 31.9 us (0.985)
  Pallas kernels: 31.5 us -> 31.1 us
    pallas_call x1, Pallas kernels: 31.5 us -> 31.1 us  [shards(): pl.pallas_call(functools.partial(cycle, n, lanes, cap), out_shape=jax.Sha...]
where the time goes in v4:
time: 31.9 us; the launch traced here: 31.8 us
  Pallas kernels  31.1 us (97%)
  local copies, waits for them, and re-layouts  0.71 us (2%)
    pallas_call x1, Pallas kernels, shards(): pl.pallas_call(functools.partial(cycle, n, lanes, cap), out_shape=jax.Sha...  31.1 us
    unnamed x1, local copies, waits for them, and re-layouts  0.71 us

profile of v4, /device:TPU:6, one launch (start us, length us, event | category | flops | bytes accessed | tf_op | source)
XLA Modules:
  0.0 31.8 jit_solution(388125755494504767)
XLA Ops:
  0.0 31.1 %cycle.1 = f32[512,128]{1,0:T(8,128)S(1)} custom-call(s32[1024]{0:T(1024)} %counts_hbm.1, f32[512,128]{1,0:T(8,128)} %b_hbm.1, f32[4,128]{1,0:T(4,128)} %bitcast.1, f32[128,128]{1,0:T(8,128)} %cell_hbm.1, f32[128,128]{1,0:T(8,128)} %near_hbm.1, f32[128,128]{1,0:T(8,128)} %far_hbm.1, f32[8,128,128]{2,1,0:T(8,128)} %prolong_hbm.1), custom_call_target="tpu_custom_call" | custom-call | tf_op jit(solution)/shard_map/cycle/pallas_call | solution.py:507
  31.1 0.7 %copy.9 = f32[512,128]{1,0:T(8,128)} copy(f32[512,128]{1,0:T(8,128)S(1)} %cycle.1) | data formatting | bytes 524288

commit v5 on v3

--- a/solution.py
+++ b/solution.py
@@ -45,7 +45,7 @@
     counts_hbm, b_hbm, coef_hbm, cell_hbm, near_hbm, far_hbm, prolong_hbm,
     out_ref,
     counts, b_own, coef, cell, near, far, prolong,
-    tail, ghost_low, ghost_high, meta, meta_in,
+    tail, ghost_low, ghost_high, meta, meta_in, coef_in,
     a_left, a_high, wide_b, wide_a, wide_j, x, d, y, res,
     strip1, strip2, strip3, strip_d,
     main_w, mix_w, rest_w, pro_w, pro_low,
@@ -85,7 +85,7 @@
                 barrier, inc=1, device_id=device(step), device_id_type=pl.DeviceIdType.MESH
             )
 
-    for step in STEPS:
+    for step in (-1, -2, -3):
         signal(step)
     loads = [
         pltpu.make_async_copy(src, dst, local_sem.at[i])
@@ -130,6 +130,25 @@
 
     live = count(me)
     c_live = lax.div(live, 8)
+    loads[2].wait()
+    tail[...] = b_own[pl.ds(8 * (c_live - left // 8), left), :]
+
+    @pl.when(me < n - 1)
+    def _():
+        pl.semaphore_wait(barrier, jnp.minimum(n - 1 - me, 3))
+
+    halo = [
+        remote(tail, ghost_low, b_send, b_recv, 0),
+        remote(b_own.at[pl.ds(0, right)], ghost_high.at[pl.ds(half, right)], b_send, b_recv, 1),
+    ]
+    raw = remote(coef, coef_in, b_send, b_recv, 0, 2)
+    start(raw)
+    early = lax.rem(lax.axis_index("sfc"), 2) == 1
+
+    @pl.when(early)
+    def _():
+        start(halo[0])
+
     for i in range(cap // 128):
         wide_a[pl.ds(left + 128 * i, 128), :] = columns(coef[pl.ds(i, 1), :])
     mean = wide_a[pl.ds(left, c_cap, stride=8), :]
@@ -141,18 +160,10 @@
     both = jnp.concatenate([mean, c_coef[pl.ds(c_live, c_cap), :]], 0)
     meta[pl.ds(0, 4), :] = coef[...]
     meta[pl.ds(4, 4), :] = jnp.transpose(both)[0:4, :]
-
-    loads[2].wait()
-    tail[...] = b_own[pl.ds(8 * (c_live - left // 8), left), :]
-    pl.semaphore_wait(barrier, jnp.minimum(me, 3) + jnp.minimum(n - 1 - me, 3))
-    halo = [
-        remote(tail, ghost_low, b_send, b_recv, 0),
-        remote(b_own.at[pl.ds(0, right)], ghost_high.at[pl.ds(half, right)], b_send, b_recv, 1),
-    ]
     metas = [
         remote(meta, meta_in.at[i], m_send, m_recv, i) for i in range(len(STEPS))
     ]
-    for c in [metas[0], halo[0], metas[1], halo[1]] + metas[2:]:
+    for c in metas[::2]:
         start(c)
 
     for c in loads[3:6]:
@@ -251,6 +262,10 @@
         x, wide_a, wide_b, left + right, inner
     )
 
+    @pl.when(jnp.logical_not(early))
+    def _():
+        start(halo[0])
+
     loads[6].wait()
     for i in range(8):
         m = prolong[i]
@@ -265,9 +280,11 @@
 
     low_limit = jnp.where(has_prev, 0, left)
     left_rows = rows_of(0, left) >= low_limit
-    received(metas[0])
+    received(raw)
+    start(metas[1])
+    start(halo[1])
     for i in range(cap // 128):
-        a_left[pl.ds(128 * i, 128), :] = columns(meta_in[0, pl.ds(i, 1), :])
+        a_left[pl.ds(128 * i, 128), :] = columns(coef_in[pl.ds(i, 1), :])
     n1 = lax.div(count(at(-1)), 8)
     a_low = jnp.where(left_rows, a_left[pl.ds(8 * (n1 - left // 8), left), :], 0.0)
     wide_a[pl.ds(0, left), :] = a_low
@@ -310,14 +327,19 @@
         remote(c_own.at[pl.ds(front, 56)], r2.at[pl.ds(72, 56)], c_send, c_recv, 3),
         remote(c_own.at[pl.ds(front, 24)], r3.at[pl.ds(104, 24)], c_send, c_recv, 5, 4),
     ]
-    for c in coarse:
+    for c in (coarse[0], coarse[2], coarse[1]):
         start(c)
     x[pl.ds(2 * stride, left), :] = strip3[pl.ds(0, left), :]
     x_head[...] = x[pl.ds(left - 2 * stride, 5 * stride), :]
     halo_x = remote(x_head, x_high.at[pl.ds(half, 5 * stride)], x_send, x_recv, 1, 0)
     start(halo_x)
-
-    for c in metas[1:]:
+    for c, other, rows in ((metas[2], metas[3], coarse[3]), (metas[4], metas[5], coarse[4])):
+        received(c)
+        start(other)
+        start(rows)
+    received(metas[0])
+
+    for c in metas[1::2]:
         received(c)
     for i in range(2):
         a_high[pl.ds(half + 128 * i, 128), :] = columns(meta_in[1, pl.ds(i, 1), :])
@@ -444,7 +466,7 @@
         low, high = low + stride, high - stride
         improve(x, d, wide_a, wide_j, wide_b, low, high, keep, gain)
     out_ref[...] = jnp.where(own_rows, x[own, :], 0.0)
-    for c in halo + metas + coarse + [halo_x]:
+    for c in halo + metas + coarse + [halo_x, raw]:
         sent(c)
 
 
@@ -466,7 +488,7 @@
         pltpu.SMEM(fine_count.shape, jnp.int32), vmem(cap, 128), vmem(4, 128),
         vmem(128, 128), vmem(128, 128), vmem(128, 128), vmem(8, 128, 128),
         vmem(left, 128), vmem(left, 128), vmem(cap + right, 128), vmem(8, 128),
-        vmem(6, 8, 128),
+        vmem(6, 8, 128), vmem(4, 128),
         vmem(cap, 128), vmem(cap + right, 128), vmem(total, 128), vmem(total, 128),
         vmem(total, 128), vmem(total + stride, 128), vmem(total, 128),
         vmem(5, total + 2 * stride, 128), vmem(cap + right + stride, 128),
@@ -482,7 +504,7 @@
     scratch += [vmem(c_total, 128)] * 3 + [vmem(c_total + stride, 128), vmem(c_total, 128)]
     scratch += [vmem(5 * stride, 128), vmem(half + 416, 128)]
     dma = pltpu.SemaphoreType.DMA
-    scratch += [dma((7,)), dma((2,)), dma((2,)), dma((6,)), dma((6,)), dma((5,)), dma((5,))]
+    scratch += [dma((7,)), dma((3,)), dma((3,)), dma((6,)), dma((6,)), dma((5,)), dma((5,))]
     scratch += [dma((1,)), dma((1,))]
     return pl.pallas_call(
         functools.partial(cycle, n, lanes, cap),

time: 32.4 us -> 30.2 us (0.932)
  Pallas kernels: 31.5 us -> 29.3 us
    pallas_call x1, Pallas kernels: 31.5 us -> 29.3 us  [shards(): pl.pallas_call(functools.partial(cycle, n, lanes, cap), out_shape=jax.Sha...]
where the time goes in v5:
time: 30.2 us; the launch traced here: 30 us
  Pallas kernels  29.3 us (97%)
  local copies, waits for them, and re-layouts  0.71 us (2%)
    pallas_call x1, Pallas kernels, shards(): pl.pallas_call(functools.partial(cycle, n, lanes, cap), out_shape=jax.Sha...  29.3 us
    unnamed x1, local copies, waits for them, and re-layouts  0.71 us

profile of v5, /device:TPU:6, one launch (start us, length us, event | category | flops | bytes accessed | tf_op | source)
XLA Modules:
  0.0 30.0 jit_solution(11166999894035058286)
XLA Ops:
  0.0 29.3 %cycle.1 = f32[512,128]{1,0:T(8,128)S(1)} custom-call(s32[1024]{0:T(1024)} %counts_hbm.1, f32[512,128]{1,0:T(8,128)} %b_hbm.1, f32[4,128]{1,0:T(4,128)} %bitcast.1, f32[128,128]{1,0:T(8,128)} %cell_hbm.1, f32[128,128]{1,0:T(8,128)} %near_hbm.1, f32[128,128]{1,0:T(8,128)} %far_hbm.1, f32[8,128,128]{2,1,0:T(8,128)} %prolong_hbm.1), custom_call_target="tpu_custom_call" | custom-call | tf_op jit(solution)/shard_map/cycle/pallas_call | solution.py:509
  29.3 0.7 %copy.9 = f32[512,128]{1,0:T(8,128)} copy(f32[512,128]{1,0:T(8,128)S(1)} %cycle.1) | data formatting | bytes 524288

commit v6 on v5

--- a/solution.py
+++ b/solution.py
@@ -85,8 +85,6 @@
                 barrier, inc=1, device_id=device(step), device_id_type=pl.DeviceIdType.MESH
             )
 
-    for step in (-1, -2, -3):
-        signal(step)
     loads = [
         pltpu.make_async_copy(src, dst, local_sem.at[i])
         for i, (src, dst) in enumerate(
@@ -98,6 +96,8 @@
     ]
     for c in loads:
         c.start()
+    for step in (-1, -2, -3):
+        signal(step)
 
     def remote(src, dst, send, recv, slot, sem=None):
         sem = slot if sem is None else sem
@@ -143,11 +143,7 @@
     ]
     raw = remote(coef, coef_in, b_send, b_recv, 0, 2)
     start(raw)
-    early = lax.rem(lax.axis_index("sfc"), 2) == 1
-
-    @pl.when(early)
-    def _():
-        start(halo[0])
+    start(halo[0])
 
     for i in range(cap // 128):
         wide_a[pl.ds(left + 128 * i, 128), :] = columns(coef[pl.ds(i, 1), :])
@@ -261,10 +257,6 @@
     res[pl.ds(2 * right, cap - right), :] = residual(
         x, wide_a, wide_b, left + right, inner
     )
-
-    @pl.when(jnp.logical_not(early))
-    def _():
-        start(halo[0])
 
     loads[6].wait()
     for i in range(8):
@@ -393,7 +385,7 @@
     r = rows_of(0, base)
     v2 = jnp.concatenate([k2[pl.ds(48 - e2, 48), :], zeros(base - 48)], 0)
     v3 = jnp.concatenate([k3[pl.ds(16 - e3, 16), :], zeros(base - 16)], 0)
-    value = jnp.where(r >= e2, k1[...], jnp.where(r >= e3, v2, v3))
+    value = jnp.where(r >= e2, k1[pl.ds(0, base), :], jnp.where(r >= e3, v2, v3))
     c_a[pl.ds(0, base), :] = jnp.where(r >= c_low, value, 0.0)
     r = rows_of(base, c_cap + base)
     v0 = jnp.concatenate([mean, zeros(base)], 0)
@@ -408,7 +400,7 @@
         c_live_rows, 1.0 / (jnp.where(c_live_rows, c_a[...], 16.0) + diag), 0.0
     )
 
-    for c in coarse:
+    for c in (coarse[1], coarse[3], coarse[4]):
         received(c)
     o1 = s1 - edge
     o2 = s2 - edge
@@ -417,13 +409,6 @@
     t2 = jnp.where(me == n - 2, c_total, o2)
     t3 = jnp.where(me == n - 3, c_total, o3)
     f2 = e2 - edge
-    r = rows_of(0, front)
-    v1 = l1[pl.ds(4, front), :]
-    v2 = jnp.concatenate([l2[pl.ds(40 - f2, 40), :], zeros(front - 40)], 0)
-    value = jnp.where(
-        r >= base - edge, c_own[pl.ds(4, front), :], jnp.where(r >= f2, v1, v2)
-    )
-    c_b[pl.ds(0, front), :] = jnp.where(r >= c_low, value, 0.0)
     r = rows_of(front, c_total - front)
     v0 = jnp.concatenate([c_own[pl.ds(front + 4, base), :], zeros(front)], 0)
     v1 = jnp.concatenate([zeros(24), r1[pl.ds(136 - o1, 128), :]], 0)
@@ -433,6 +418,15 @@
     c_b[pl.ds(front, c_total - front), :] = jnp.where(
         (r >= c_low) & (r < c_high), value, 0.0
     )
+    for c in (coarse[2], coarse[0]):
+        received(c)
+    r = rows_of(0, front)
+    v1 = l1[pl.ds(4, front), :]
+    v2 = jnp.concatenate([l2[pl.ds(40 - f2, 40), :], zeros(front - 40)], 0)
+    value = jnp.where(
+        r >= base - edge, c_own[pl.ds(4, front), :], jnp.where(r >= f2, v1, v2)
+    )
+    c_b[pl.ds(0, front), :] = jnp.where(r >= c_low, value, 0.0)
     first = c_j[...] * c_b[...] * (1.0 / CENTER)
     c_x[pl.ds(0, c_total), :] = first
     c_d[...] = first
@@ -491,16 +485,16 @@
         vmem(6, 8, 128), vmem(4, 128),
         vmem(cap, 128), vmem(cap + right, 128), vmem(total, 128), vmem(total, 128),
         vmem(total, 128), vmem(total + stride, 128), vmem(total, 128),
-        vmem(5, total + 2 * stride, 128), vmem(cap + right + stride, 128),
+        vmem(5, total + 2 * stride, 128), vmem(cap + right + stride + 8, 128),
         vmem(9 * stride, 128), vmem(9 * stride, 128), vmem(9 * stride, 128),
         vmem(8 * stride, 128),
         vmem(256, 768, dtype=BF16), vmem(256, 256, dtype=BF16),
         vmem(2048, 256, dtype=BF16),
         vmem(256, 1024, dtype=BF16), vmem(128, 1024, dtype=BF16),
-        vmem(160, 128), vmem(c_cap, 128), vmem(2 * c_cap, 128),
+        vmem(168, 128), vmem(c_cap, 128), vmem(2 * c_cap + 8, 128),
         vmem(88, 128), vmem(80, 128), vmem(168, 128), vmem(168, 128), vmem(168, 128),
     ]
-    scratch += [vmem(base, 128)] * 3 + [vmem(base + c_cap, 128)] * 3
+    scratch += [vmem(base + 8, 128)] * 3 + [vmem(base + c_cap + 8, 128)] * 3
     scratch += [vmem(c_total, 128)] * 3 + [vmem(c_total + stride, 128), vmem(c_total, 128)]
     scratch += [vmem(5 * stride, 128), vmem(half + 416, 128)]
     dma = pltpu.SemaphoreType.DMA

time: 30.2 us -> 30.1 us (level)
  no operation moved by 1% of the time
where the time goes in v6:
time: 30.1 us; the launch traced here: 30 us
  Pallas kernels  29.3 us (97%)
  local copies, waits for them, and re-layouts  0.71 us (2%)
    pallas_call x1, Pallas kernels, shards(): pl.pallas_call(functools.partial(cycle, n, lanes, cap), out_shape=jax.Sha...  29.3 us
    unnamed x1, local copies, waits for them, and re-layouts  0.71 us

profile of v6, /device:TPU:6, one launch (start us, length us, event | category | flops | bytes accessed | tf_op | source)
XLA Modules:
  0.0 30.0 jit_solution(789225378670002668)
XLA Ops:
  0.0 29.3 %cycle.1 = f32[512,128]{1,0:T(8,128)S(1)} custom-call(s32[1024]{0:T(1024)} %counts_hbm.1, f32[512,128]{1,0:T(8,128)} %b_hbm.1, f32[4,128]{1,0:T(4,128)} %bitcast.1, f32[128,128]{1,0:T(8,128)} %cell_hbm.1, f32[128,128]{1,0:T(8,128)} %near_hbm.1, f32[128,128]{1,0:T(8,128)} %far_hbm.1, f32[8,128,128]{2,1,0:T(8,128)} %prolong_hbm.1), custom_call_target="tpu_custom_call" | custom-call | tf_op jit(solution)/shard_map/cycle/pallas_call | solution.py:503
  29.3 0.7 %copy.9 = f32[512,128]{1,0:T(8,128)} copy(f32[512,128]{1,0:T(8,128)S(1)} %cycle.1) | data formatting | bytes 524288
